TPU v7x, 32 devices: a whole 2x2x4 slice. The times are simulated.
32 devices in a mesh: gx: 8 (over z, x), gy: 4 (over y, core).
Axes of the slice: x: 2, y: 2, z: 4, core: 2. Of those that a mesh axis runs over, the one named last changes fastest.
Arguments:
- pressure: float32 [256, 128, 128], P('gx', 'gy'), may hold values from -6 to 6
- depth: float32 [256, 128, 128], P('gx', 'gy'), may hold values from -6 to 6
- saturation: float32 [2, 256, 128, 128], P(None, 'gx', 'gy'), may hold values from 0.05 to 0.45
- permeability: float32 [3, 256, 128, 128], P(None, 'gx', 'gy'), may hold values from 0.1 to 10
- pore_volume: float32 [256, 128, 128], P('gx', 'gy'), may hold values from 0.5 to 2
- fault_pairs: int32 [1024, 3], P(('gx', 'gy')), may hold values from 0 to 1023, as said below
- fault_kind: int32 [1024], P(('gx', 'gy')), may hold values from 0 to 15
- fault_count: int32 [32], P(('gx', 'gy')), may hold values from 8 to 32, as said below
- fault_table: float32 [16, 128], replicated, may hold values from 0.2 to 2
Outputs:
- saturation_next: float32 [3, 256, 128, 128], P(None, 'gx', 'gy')
Inputs may be any that keep to these rules, and one draw needn't show every extreme that they name: `fault_pairs`: each device holds 32 rows. Column 0 and column 2 are areal column numbers a * 32 + b of the source and target device. Column 1 is the target device i2 * 4 + j2, which lies within one index of the source device along gx and along gy, counted cyclically. Among one device's 32 rows at most 4 name the same target device, and on every device some target device is named by exactly 4 rows. Rows 0 to fault_count - 1 of a device are live; some device has 32 live rows.
All inputs are finite; a program needn't handle non-finite values.
Results may differ from a plain program's by a relative error of at most 0.0003.
Values sent between devices are 32-bit elements; how exact they have to be, the bound alone decides.
No kernel may reach another device: no remote copies, remote signals or barrier semaphores. Data moves between devices by JAX's collectives and lax.ppermute only.
A program may use at most 64 MiB of HBM per device.

v0:
```python
import functools

import jax
import jax.numpy as jnp
from jax import lax
from jax.experimental import pallas as pl
from jax.experimental.pallas import tpu as pltpu
from jax.sharding import PartitionSpec as P


CAP = 4
FIELDS = 5
BLOCK = CAP * FIELDS
META = 3 * BLOCK
ROWS = 64
FLOW = 3 * CAP
BACK = 40

VISCOSITY = (0.5, 1.0, 0.25)
DENSITY = (1.0, 0.8, 0.25)
STEP = 0.2


VMEM = pltpu.VMEM
HBM = pltpu.HBM
SMEM = pltpu.SMEM


def spec(space):
    return pl.BlockSpec(memory_space=space)


def params(limit=6):
    return pltpu.CompilerParams(vmem_limit_bytes=limit * 2**20)


def cost(flops):
    return pl.CostEstimate(flops=flops, bytes_accessed=flops // 64, transcendentals=0)


def mobility(water, oil):
    gas = 1.0 - water - oil
    return (
        water * water * (1.0 / VISCOSITY[0]),
        oil * oil * (1.0 / VISCOSITY[1]),
        gas * gas * (1.0 / VISCOSITY[2]),
    )


def harmonic(first, second):
    return (first * second + first * second) / (first + second)


def flux(low, high, trans):
    dp = low[0] - high[0]
    dd = low[1] - high[1]
    flows = []
    for phase in range(3):
        drive = dp - DENSITY[phase] * dd if DENSITY[phase] != 1.0 else dp - dd
        up = jnp.where(drive > 0.0, low[2 + phase], high[2 + phase])
        flows.append(trans * drive * up)
    return flows


def pack_kernel(
    nx, ny,
    pairs_ref, kind_ref, count_ref, table_ref, press_f, depth_f, sat_f,
    own, msg_a, msg_b, press, depth, sat,
    pairs_s, kind_s, count_s, slot_s, seen_s, src_s, knd_s, liv_s, lnd_s, table,
    sem_i, sem_s,
):
    ints = [
        pltpu.make_async_copy(pairs_ref, pairs_s, sem_i.at[0]),
        pltpu.make_async_copy(kind_ref, kind_s, sem_i.at[1]),
        pltpu.make_async_copy(count_ref, count_s, sem_i.at[2]),
        pltpu.make_async_copy(table_ref, table, sem_i.at[3]),
    ]
    for copy in ints:
        copy.start()
    bulk = [
        pltpu.make_async_copy(press_f, press, sem_s.at[0]),
        pltpu.make_async_copy(depth_f, depth, sem_s.at[1]),
        pltpu.make_async_copy(sat_f, sat, sem_s.at[2]),
    ]
    for copy in bulk:
        copy.start()
    home_x = lax.axis_index("gx")
    home_y = lax.axis_index("gy")
    even_y = lax.rem(home_y, 2) == 0
    for step_x in (0, 1, -1):
        to_x = lax.rem(home_x + step_x + nx, nx)
        tx = step_x % 3
        for step_y in (0, 1, -1):
            to_y = lax.rem(home_y + step_y + ny, ny)
            if step_y == 0:
                ty = 0
            else:
                ty = jnp.where(even_y == (step_y == 1), 1, 2)
            slot_s[to_x * ny + to_y] = (ty * 3 + tx) * CAP
    for k in range(9 * CAP):
        seen_s[k] = 0
        src_s[k] = 0
        knd_s[k] = 0
        liv_s[k] = 0
        lnd_s[k] = 0
    for copy in ints:
        copy.wait()
    count = count_s[0, 0]
    for r in range(pairs_s.shape[1]):
        base = slot_s[pairs_s[1, r]]
        rank = seen_s[base]
        seen_s[base] = rank + 1
        position = base + rank
        src_s[position] = pairs_s[0, r]
        lnd_s[position] = pairs_s[2, r]
        knd_s[position] = kind_s[r]
        liv_s[position] = jnp.where(r < count, 1, 0)
    lane = lax.broadcasted_iota(jnp.int32, (1, own.shape[1]), 1)
    messages = (own, msg_a, msg_b)
    origin = jnp.zeros(lane.shape, jnp.int32)
    for ty in range(3):
        out = messages[ty]
        for tx in range(3):
            meta = jnp.zeros(lane.shape, jnp.int32)
            for rank in range(CAP):
                k = (ty * 3 + tx) * CAP + rank
                meta = jnp.where(lane == rank, lnd_s[k], meta)
                origin = jnp.where(lane == k, src_s[k], origin)
                trans = table[pl.ds(knd_s[k], 1), :]
                alive = liv_s[k].astype(jnp.float32)
                out[tx * BLOCK + 4 * CAP + rank : tx * BLOCK + 4 * CAP + rank + 1, :] = trans * alive
            out[META + tx : META + tx + 1, :] = meta.astype(jnp.float32)
        out[META + 3 : META + 4, :] = jnp.zeros(lane.shape, jnp.float32)
    own[META + 3 : META + 4, :] = origin.astype(jnp.float32)
    for copy in bulk:
        copy.wait()
    for ty in range(3):
        out = messages[ty]
        for tx in range(3):
            for rank in range(CAP):
                k = (ty * 3 + tx) * CAP + rank
                col = src_s[k]
                at = tx * BLOCK + rank
                out[at : at + 1, :] = press[pl.ds(col, 1), :]
                out[at + CAP : at + CAP + 1, :] = depth[pl.ds(col, 1), :]
                out[at + 2 * CAP : at + 2 * CAP + 1, :] = sat[0, pl.ds(col, 1), :]
                out[at + 3 * CAP : at + 3 * CAP + 1, :] = sat[1, pl.ds(col, 1), :]


def load_state(press, depth, sat, rows):
    water, oil = sat[0, rows, :], sat[1, rows, :]
    return (press[rows, :], depth[rows, :]) + mobility(water, oil), water, oil


def stencil_kernel(cx, cy, first, last, *refs):
    if first == 0:
        press, depth, sat, perm, pore, out = refs
    else:
        press, depth, sat, perm, pore, _, out = refs
    lanes = press.shape[1]
    lane = lax.broadcasted_iota(jnp.int32, (8, lanes), 1)
    sub = lax.broadcasted_iota(jnp.int32, (8, lanes), 0)
    chunks = cy // 8

    def at(a, c, shift=0):
        return pl.ds(pl.multiple_of(a * cy, 8) + (c * 8 + shift), 8)

    def flow_x(a, c, low):
        rows = at(a + 1, c)
        high, _, _ = load_state(press, depth, sat, rows)
        trans = harmonic(perm[0, at(a, c), :], perm[0, rows, :])
        return flux(low, high, trans)

    def one_row(a, carry, top):
        out_carry = []
        below = None
        for c in range(chunks):
            rows = at(a, c)
            mine, water, oil = load_state(press, depth, sat, rows)
            if top:
                net = [-carry[3 * c + f] for f in range(3)]
            else:
                up = flow_x(a, c, mine)
                out_carry += up
                net = [up[f] - carry[3 * c + f] for f in range(3)]
            ky = perm[1, rows, :]
            if c < chunks - 1:
                rows_up = at(a, c, 1)
                high, _, _ = load_state(press, depth, sat, rows_up)
                trans = harmonic(ky, perm[1, rows_up, :])
            else:
                high = tuple(pltpu.roll(v, 7, 0) for v in mine)
                trans = jnp.where(sub < 7, harmonic(ky, pltpu.roll(ky, 7, 0)), 0.0)
            flow = flux(mine, high, trans)
            for f in range(3):
                back = pltpu.roll(flow[f], 1, 0)
                first_row = jnp.zeros_like(back) if c == 0 else below[f]
                net[f] = net[f] + (flow[f] - jnp.where(sub == 0, first_row, back))
            below = [pltpu.roll(flow[f], 1, 0) for f in range(3)]
            kz = perm[2, rows, :]
            high = tuple(pltpu.roll(v, lanes - 1, 1) for v in mine)
            trans = jnp.where(lane < lanes - 1, harmonic(kz, pltpu.roll(kz, lanes - 1, 1)), 0.0)
            flow = flux(mine, high, trans)
            for f in range(3):
                net[f] = net[f] + (flow[f] - pltpu.roll(flow[f], 1, 1))
            scale = STEP / pore[rows, :]
            gas = 1.0 - water - oil
            for f, now in enumerate((water, oil, gas)):
                out[f, rows, :] = now - scale * net[f]
        return tuple(out_carry)

    if first == 0:
        carry = tuple(jnp.zeros((8, lanes), jnp.float32) for _ in range(3 * chunks))
    else:
        carry = []
        for c in range(chunks):
            low, _, _ = load_state(press, depth, sat, at(first - 1, c))
            carry += flow_x(first - 1, c, low)
        carry = tuple(carry)
    end = min(last, cx - 1)
    carry = lax.fori_loop(first, end, lambda a, value: one_row(a, value, False), carry)
    if last == cx:
        one_row(cx - 1, carry, True)


def halo_kernel(cx, cy, press, depth, sat, perm, _, hxa, hxb, hya, hyb):
    even_x = lax.rem(lax.axis_index("gx"), 2) == 0
    even_y = lax.rem(lax.axis_index("gy"), 2) == 0
    columns = cx * cy
    low, high = pl.ds(0, cy), pl.ds(columns - cy, cy)
    left, right = pl.ds(0, cx, stride=cy), pl.ds(cy - 1, cx, stride=cy)
    for field in range(5):

        def rows(where, dim):
            if field < 2:
                return (press, depth)[field][where, :]
            return sat[field - 2, where, :] if field < 4 else perm[dim, where, :]

        first, last = rows(low, 0), rows(high, 0)
        hxa[field] = jnp.where(even_x, last, first)
        hxb[field] = jnp.where(even_x, first, last)
        first, last = rows(left, 1), rows(right, 1)
        hya[field] = jnp.where(even_y, last, first)
        hyb[field] = jnp.where(even_y, first, last)


def blocks_of(own, got_a, got_b, plus, minus):
    listing = [(own, 0), (got_a, 0), (got_b, 0)]
    listing += [(plus, b) for b in range(3)] + [(minus, b) for b in range(3)]
    return listing


def fault_kernel(
    own, got_a, got_b, plus, minus, press, depth, sat, _,
    back_plus, back_minus, back_y, local,
):
    listing = blocks_of(own, got_a, got_b, plus, minus)
    targets = [(back_y, k * FLOW) for k in range(3)]
    targets += [(back_plus, k * FLOW) for k in range(3)]
    targets += [(back_minus, k * FLOW) for k in range(3)]
    for n, (ref, block) in enumerate(listing):
        meta = ref[META + block : META + block + 1, :].astype(jnp.int32)
        for rank in range(CAP):
            col = meta[0, rank]
            at = n * 4 * CAP + rank
            local[at : at + 1, :] = press[pl.ds(col, 1), :]
            local[at + CAP : at + CAP + 1, :] = depth[pl.ds(col, 1), :]
            local[at + 2 * CAP : at + 2 * CAP + 1, :] = sat[0, pl.ds(col, 1), :]
            local[at + 3 * CAP : at + 3 * CAP + 1, :] = sat[1, pl.ds(col, 1), :]
    for n, (ref, block) in enumerate(listing):
        far = [ref[block * BLOCK + f * CAP : block * BLOCK + (f + 1) * CAP, :] for f in range(5)]
        near = [local[(n * 4 + f) * CAP : (n * 4 + f + 1) * CAP, :] for f in range(4)]
        flow = flux(
            (far[0], far[1]) + mobility(far[2], far[3]),
            (near[0], near[1]) + mobility(near[2], near[3]),
            far[4],
        )
        out, row = targets[n]
        for f in range(3):
            out[row + f * CAP : row + (f + 1) * CAP, :] = flow[f]
    for out in (back_plus, back_minus, back_y):
        out[3 * FLOW : BACK, :] = jnp.zeros((BACK - 3 * FLOW, out.shape[1]), jnp.float32)


def edge_kernel(
    nx, ny, cx, cy,
    own, got_a, got_b, plus, minus, back_plus, back_minus, back_y,
    hxa, hxb, hya, hyb, press, depth, sat, perm, pore, _,
    out,
):
    listing = blocks_of(own, got_a, got_b, plus, minus)
    sources = [(back_y, k * FLOW) for k in range(3)]
    sources += [(back_plus, k * FLOW) for k in range(3)]
    sources += [(back_minus, k * FLOW) for k in range(3)]
    home_x = lax.axis_index("gx")
    home_y = lax.axis_index("gy")
    columns = cx * cy

    def edge(first, second, dim, home, ends, rows_low, rows_high):
        even = lax.rem(home, 2) == 0
        for is_upper, rows in ((True, rows_high), (False, rows_low)):
            pick = even if is_upper else jnp.logical_not(even)
            far = [jnp.where(pick, first[f], second[f]) for f in range(5)]
            exists = (home < ends - 1) if is_upper else (home > 0)
            there = jnp.where(exists, 1.0, 0.0)
            mine, _, _ = load_state(press, depth, sat, rows)
            other = (far[0], far[1]) + mobility(far[2], far[3])
            trans = harmonic(perm[dim, rows, :], far[4]) * there
            if is_upper:
                flow = flux(mine, other, trans)
            else:
                flow = [-v for v in flux(other, mine, trans)]
            scale = STEP / pore[rows, :]
            for f in range(3):
                out[f, rows, :] = out[f, rows, :] - scale * flow[f]

    edge(hxa, hxb, 0, home_x, nx, pl.ds(0, cy), pl.ds(columns - cy, cy))
    edge(hya, hyb, 1, home_y, ny, pl.ds(0, cx, stride=cy), pl.ds(cy - 1, cx, stride=cy))
    for n, (ref, block) in enumerate(listing):
        meta = ref[META + block : META + block + 1, :].astype(jnp.int32)
        flows, row = sources[n]
        for rank in range(CAP):
            col = meta[0, rank]
            scale = STEP / pore[pl.ds(col, 1), :]
            for f in range(3):
                at = row + f * CAP + rank
                out[f, pl.ds(col, 1), :] = out[f, pl.ds(col, 1), :] + scale * flows[at : at + 1, :]


def finish_kernel(own, back_y, from_up, from_down, from_a, from_b, pore, _, out, work, sem):
    origin = own[META + 3 : META + 4, :].astype(jnp.int32)
    for ty in range(3):
        for tx in range(3):
            if ty > 0:
                ref, row = (from_a, from_b)[ty - 1], tx * FLOW
            elif tx == 0:
                ref, row = back_y, 0
            else:
                ref, row = (from_up, from_down)[tx - 1], 0
            for rank in range(CAP):
                col = origin[0, (ty * 3 + tx) * CAP + rank]
                scale = STEP / pore[pl.ds(col, 1), :]
                for f in range(3):
                    at = row + f * CAP + rank
                    work[f, pl.ds(col, 1), :] = (
                        work[f, pl.ds(col, 1), :] - scale * ref[at : at + 1, :]
                    )
    copy = pltpu.make_async_copy(work, out, sem)
    copy.start()
    copy.wait()


def swapped(value, axis, kind):
    count = lax.axis_size(axis)
    route = []
    for i in range(count):
        j = i ^ 1 if kind == 0 else (((i + 1) ^ 1) - 1) % count
        route.append((i, j))
    return lax.ppermute(value, axis, route)


def swapped_inside(value):
    nx, ny = lax.axis_size("gx"), lax.axis_size("gy")
    route = []
    for i in range(nx):
        for j in range(ny):
            if i in (0, nx - 1):
                route.append((i * ny + j, i * ny + (j ^ 1)))
            else:
                route.append((i * ny + j, (((i + 1) ^ 1) - 1) * ny + j))
    return lax.ppermute(value, ("gx", "gy"), route)


def shifted(value, axis, step):
    count = lax.axis_size(axis)
    return lax.ppermute(value, axis, [(i, (i + step) % count) for i in range(count)])


def relay_kernel(own, got_a, got_b, _, plus, minus):
    parts = (own, got_a, got_b)
    for tx, out in ((1, plus), (2, minus)):
        low = tx * BLOCK
        for k, part in enumerate(parts):
            out[k * BLOCK : (k + 1) * BLOCK, :] = part[low : low + BLOCK, :]
            out[META + k : META + k + 1, :] = part[META + tx : META + tx + 1, :]
        out[META + 3 :, :] = jnp.zeros((1, out.shape[1]), jnp.float32)


def relay_back_kernel(back_y, from_up, from_down, _, back_a, back_b):
    for ty, out in ((1, back_a), (2, back_b)):
        low = ty * FLOW
        for k, part in enumerate((back_y, from_up, from_down)):
            out[k * FLOW : (k + 1) * FLOW, :] = part[low : low + FLOW, :]
        out[3 * FLOW :, :] = jnp.zeros((BACK - 3 * FLOW, out.shape[1]), jnp.float32)


def step(
    pressure, depth, saturation, permeability, pore_volume,
    fault_pairs, fault_kind, fault_count, fault_table,
):
    cx, cy, layers = pressure.shape
    columns = cx * cy
    nx, ny = lax.axis_size("gx"), lax.axis_size("gy")
    f32 = jnp.float32
    slots = 9 * CAP
    rows = fault_pairs.shape[0]

    def flat(array):
        return array.reshape(array.shape[:-3] + (columns, layers))

    def cells(array):
        return array.reshape(array.shape[:-2] + (cx, cy, layers))

    def outer(array):
        return pltpu.with_memory_space_constraint(array, HBM)

    def vmem(*dims):
        return VMEM(dims, f32)

    message, back, full = vmem(ROWS, layers), vmem(BACK, layers), vmem(3, columns, layers)
    halo_x, halo_y = vmem(5, cy, layers), vmem(5, cx, layers)
    own, msg_a, msg_b, press, deep, sat = pl.pallas_call(
        functools.partial(pack_kernel, nx, ny),
        in_specs=[spec(HBM)] * 7,
        out_specs=[spec(VMEM)] * 6,
        out_shape=[message] * 3
        + [vmem(columns, layers)] * 2 + [vmem(2, columns, layers)],
        scratch_shapes=[
            SMEM((3, rows), jnp.int32), SMEM((rows,), jnp.int32), SMEM((1, 1), jnp.int32),
            SMEM((nx * ny,), jnp.int32),
            SMEM((slots,), jnp.int32), SMEM((slots,), jnp.int32), SMEM((slots,), jnp.int32),
            SMEM((slots,), jnp.int32), SMEM((slots,), jnp.int32),
            VMEM(fault_table.shape, f32),
            pltpu.SemaphoreType.DMA((4,)), pltpu.SemaphoreType.DMA((3,)),
        ],
        compiler_params=params(),
        cost_estimate=cost(4_000_000),
        name="pack",
    )(*map(lambda a: a if a.size <= 1 else outer(a), (
        fault_pairs.T, fault_kind, fault_count.reshape(1, 1), fault_table,
        flat(pressure), flat(depth), flat(saturation),
    )))
    perm, pore = flat(permeability), flat(pore_volume)

    cuts = tuple(cx * k // 4 for k in range(5))

    def stencil(part, base):
        first, last = cuts[part], cuts[part + 1]
        operands = [press, deep, sat, perm, pore] + ([] if first == 0 else [base])
        return pl.pallas_call(
            functools.partial(stencil_kernel, cx, cy, first, last),
            in_specs=[spec(VMEM)] * 5 + ([] if first == 0 else [spec(pl.ANY)]),
            out_specs=spec(VMEM),
            out_shape=full,
            input_output_aliases={} if first == 0 else {5: 0},
            compiler_params=params(),
            cost_estimate=cost(8_000_000 * (last - first) // 8),
        )(*operands)

    got_a = swapped(msg_a, "gy", 0)
    got_b = swapped(msg_b, "gy", 1)
    base = stencil(0, None)
    plus, minus = pl.pallas_call(
        relay_kernel,
        in_specs=[spec(VMEM)] * 3 + [spec(pl.ANY)],
        out_specs=[spec(VMEM)] * 2,
        out_shape=[message] * 2,
        compiler_params=params(),
        cost_estimate=cost(100_000),
        name="relay",
    )(own, got_a, got_b, base)
    plus = shifted(plus, "gx", 1)
    minus = shifted(minus, "gx", -1)
    base = stencil(1, base)
    back_plus, back_minus, back_y = pl.pallas_call(
        fault_kernel,
        in_specs=[spec(VMEM)] * 8 + [spec(pl.ANY)],
        out_specs=[spec(VMEM)] * 3,
        out_shape=[back] * 3,
        scratch_shapes=[VMEM((slots * 4, layers), f32)],
        compiler_params=params(),
        cost_estimate=cost(2_000_000),
        name="fault",
    )(own, got_a, got_b, plus, minus, press, deep, sat, base)
    from_down = shifted(back_minus, "gx", 1)
    from_up = shifted(back_plus, "gx", -1)
    hxa, hxb, hya, hyb = pl.pallas_call(
        functools.partial(halo_kernel, cx, cy),
        in_specs=[spec(VMEM)] * 4 + [spec(pl.ANY)],
        out_specs=[spec(VMEM)] * 4,
        out_shape=[halo_x] * 2 + [halo_y] * 2,
        compiler_params=params(),
        cost_estimate=cost(100_000),
        name="halo",
    )(press, deep, sat, perm, back_y)
    hxa = swapped(hxa, "gx", 0)
    hxb = swapped_inside(hxb)
    hya = swapped(hya, "gy", 0)
    hyb = swapped(hyb, "gy", 1)
    base = stencil(2, base)
    back_a, back_b = pl.pallas_call(
        relay_back_kernel,
        in_specs=[spec(VMEM)] * 3 + [spec(pl.ANY)],
        out_specs=[spec(VMEM)] * 2,
        out_shape=[back] * 2,
        compiler_params=params(),
        cost_estimate=cost(100_000),
        name="relay_back",
    )(back_y, from_up, from_down, base)
    from_a = swapped(back_a, "gy", 0)
    from_b = swapped(back_b, "gy", 1)
    base = stencil(3, base)
    base = pl.pallas_call(
        functools.partial(edge_kernel, nx, ny, cx, cy),
        in_specs=[spec(VMEM)] * 18,
        out_specs=spec(VMEM),
        out_shape=full,
        input_output_aliases={17: 0},
        compiler_params=params(),
        cost_estimate=cost(4_000_000),
        name="edge",
    )(own, got_a, got_b, plus, minus, back_plus, back_minus, back_y,
      hxa, hxb, hya, hyb, press, deep, sat, perm, pore, base)
    out, _ = pl.pallas_call(
        finish_kernel,
        in_specs=[spec(VMEM)] * 8,
        out_specs=[spec(HBM), spec(VMEM)],
        out_shape=[jax.ShapeDtypeStruct((3, columns, layers), f32), full],
        input_output_aliases={7: 1},
        scratch_shapes=[pltpu.SemaphoreType.DMA],
        compiler_params=params(),
        cost_estimate=cost(2_000_000),
        name="finish",
    )(own, back_y, from_up, from_down, from_a, from_b, pore, base)
    return cells(out)


def solution(mesh):
    in_specs = (
        P("gx", "gy", None),
        P("gx", "gy", None),
        P(None, "gx", "gy", None),
        P(None, "gx", "gy", None),
        P("gx", "gy", None),
        P(("gx", "gy"), None),
        P(("gx", "gy")),
        P(("gx", "gy")),
        P(),
    )
    out_specs = P(None, "gx", "gy", None)
    return jax.shard_map(step, mesh=mesh, in_specs=in_specs, out_specs=out_specs, check_vma=False)
```

profile of v0, /device:TPU:0, one launch (start us, length us, event | category | flops | bytes accessed | tf_op | source)
XLA Modules:
  0.0 34.0 jit_solution(13734438414851341431)
XLA Ops:
  0.8 1.7 %pack.1 = (f32[64,128]{1,0:T(8,128)S(1)}, f32[64,128]{1,0:T(8,128)S(1)}, f32[64,128]{1,0:T(8,128)S(1)}, f32[1024,128]{1,0:T(8,128)S(1)}, f32[1024,128]{1,0:T(8,128)S(1)}, /*index=5*/f32[2,1024,128]{2,1,0:T(8,128)S(1)}) custom-call(s32[3,32]{1,0:T(4,128)} %bitcast.24, s32[32]{0:T(128)} %kind_ref.1, s32[1,1]{1,0:T(1,128)} %bitcast.8.count_ref, ...), custom_call_target="tpu_custom_call" | custom-call | flops 4000000 | bytes 62500 | tf_op jit(solution)/shard_map/pack/pallas_call | solution.py:422
  2.5 0.6 %collective-permute-start = (f32[64,128]{1,0:T(8,128)S(1)}, f32[64,128]{1,0:T(8,128)S(1)}, u32[]{:S(2)}, u32[]{:S(2)}) collective-permute-start(f32[64,128]{1,0:T(8,128)S(1)} %get-tuple-element.24), channel_id=1, source_target_pairs={{0,1},{1,0},{2,3},{3,2},{4,5},{5,4},{6,7},{7,6},{8,9},{9,8},{10,11... | collective-permute-start | bytes 98312 | tf_op jit(solution)/shard_map/ppermute | solution.py:359
  3.1 2.6 %collective-permute-start.1 = (f32[64,128]{1,0:T(8,128)S(1)}, f32[64,128]{1,0:T(8,128)S(1)}, u32[]{:S(2)}, u32[]{:S(2)}) collective-permute-start(f32[64,128]{1,0:T(8,128)S(1)} %get-tuple-element.25), channel_id=1, source_target_pairs={{0,3},{1,2},{2,1},{3,0},{4,7},{5,6},{6,5},{7,4},{8,11},{9,10},{10,... | collective-permute-start | bytes 98312 | tf_op jit(solution)/shard_map/ppermute | solution.py:359
  5.7 1.3 %shard_map.91._.refs_5_ = f32[3,1024,128]{2,1,0:T(8,128)S(1)} custom-call(f32[1024,128]{1,0:T(8,128)S(1)} %get-tuple-element.26.refs_0_.press, f32[1024,128]{1,0:T(8,128)S(1)} %get-tuple-element.27.refs_1_.depth, f32[2,1024,128]{2,1,0:T(8,128)S(1)} %get-tuple-element.28.refs_2_.sat, f32[3,1024,128]{2,1,0:T(8,128)S(1)} %bitcast.9, f32[1024,128]{1,0:T(8,128)S(1)} %bitcast.15), custom_call_target="tpu_custom_call" | custom-call | flops 8000000 | bytes 125000 | tf_op jit(solution)/shard_map/pallas_call | solution.py:450
  7.0 0.0 collective-permute-done.got_a
  7.1 0.3 collective-permute-done.1.got_b
  7.4 1.6 %collective-permute-start.2 = (f32[64,128]{1,0:T(8,128)S(1)}, f32[64,128]{1,0:T(8,128)S(1)}, u32[]{:S(2)}, u32[]{:S(2)}) collective-permute-start(f32[64,128]{1,0:T(8,128)S(1)} %get-tuple-element.29), channel_id=1, source_target_pairs={{0,4},{4,8},{8,12},{12,16},{16,20},{20,24},{24,28},{28,0},{1,5},{5... | collective-permute-start | bytes 98312 | tf_op jit(solution)/shard_map/ppermute | solution.py:376
  9.0 3.1 %collective-permute-start.3 = (f32[64,128]{1,0:T(8,128)S(1)}, f32[64,128]{1,0:T(8,128)S(1)}, u32[]{:S(2)}, u32[]{:S(2)}) collective-permute-start(f32[64,128]{1,0:T(8,128)S(1)} %get-tuple-element.30), channel_id=1, source_target_pairs={{0,28},{4,0},{8,4},{12,8},{16,12},{20,16},{24,20},{28,24},{1,29},{... | collective-permute-start | bytes 98312 | tf_op jit(solution)/shard_map/ppermute | solution.py:376
  12.2 1.4 %shard_map.92._.refs_5_ = f32[3,1024,128]{2,1,0:T(8,128)S(1)} custom-call(f32[1024,128]{1,0:T(8,128)S(1)} %get-tuple-element.26.refs_0_.press, f32[1024,128]{1,0:T(8,128)S(1)} %get-tuple-element.27.refs_1_.depth, f32[2,1024,128]{2,1,0:T(8,128)S(1)} %get-tuple-element.28.refs_2_.sat, f32[3,1024,128]{2,1,0:T(8,128)S(1)} %bitcast.10, ...), custom_call_target="tpu_custom_call", output_to_operand_aliasing={{}: (5, {})} | custom-call | flops 8000000 | bytes 125000 | tf_op jit(solution)/shard_map/pallas_call | solution.py:450
  13.5 0.5 %collective-permute-done.2.plus = f32[64,128]{1,0:T(8,128)S(1)} collective-permute-done((f32[64,128]{1,0:T(8,128)S(1)}, f32[64,128]{1,0:T(8,128)S(1)}, u32[]{:S(2)}, u32[]{:S(2)}) %collective-permute-start.2) | collective-permute-done | bytes 32800 | tf_op jit(solution)/shard_map/ppermute | solution.py:376
  14.1 0.0 collective-permute-done.3.minus
  14.1 0.2 fault.1
  14.3 0.1 halo.1
  14.4 1.4 %collective-permute-start.8 = (f32[5,32,128]{2,1,0:T(8,128)S(1)}, f32[5,32,128]{2,1,0:T(8,128)S(1)}, u32[]{:S(2)}, u32[]{:S(2)}) collective-permute-start(f32[5,32,128]{2,1,0:T(8,128)S(1)} %get-tuple-element.36), channel_id=1, source_target_pairs={{0,4},{4,0},{8,12},{12,8},{16,20},{20,16},{24,28},{28,24},{1,5},{5... | collective-permute-start | bytes 245768 | tf_op jit(solution)/shard_map/ppermute | solution.py:359
  15.8 0.0 collective-permute-start.9
  15.8 0.5 %collective-permute-start.10 = (f32[5,32,128]{2,1,0:T(8,128)S(1)}, f32[5,32,128]{2,1,0:T(8,128)S(1)}, u32[]{:S(2)}, u32[]{:S(2)}) collective-permute-start(f32[5,32,128]{2,1,0:T(8,128)S(1)} %get-tuple-element.38), channel_id=1, source_target_pairs={{0,1},{1,0},{2,3},{3,2},{4,5},{5,4},{6,7},{7,6},{8,9},{9,8},{10,11... | collective-permute-start | bytes 245768 | tf_op jit(solution)/shard_map/ppermute | solution.py:359
  16.3 1.1 %collective-permute-start.11 = (f32[5,32,128]{2,1,0:T(8,128)S(1)}, f32[5,32,128]{2,1,0:T(8,128)S(1)}, u32[]{:S(2)}, u32[]{:S(2)}) collective-permute-start(f32[5,32,128]{2,1,0:T(8,128)S(1)} %get-tuple-element.39), channel_id=1, source_target_pairs={{0,3},{1,2},{2,1},{3,0},{4,7},{5,6},{6,5},{7,4},{8,11},{9,10},{10,... | collective-permute-start | bytes 245768 | tf_op jit(solution)/shard_map/ppermute | solution.py:359
  17.4 3.6 %collective-permute-start.4 = (f32[40,128]{1,0:T(8,128)S(1)}, f32[40,128]{1,0:T(8,128)S(1)}, u32[]{:S(2)}, u32[]{:S(2)}) collective-permute-start(f32[40,128]{1,0:T(8,128)S(1)} %get-tuple-element.32.back_plus), channel_id=1, source_target_pairs={{0,28},{4,0},{8,4},{12,8},{16,12},{20,16},{24,20},{28,24},{1,29},{... | collective-permute-start | bytes 61448 | tf_op jit(solution)/shard_map/ppermute | solution.py:376
  21.1 1.5 %collective-permute-done.4.from_up = f32[40,128]{1,0:T(8,128)S(1)} collective-permute-done((f32[40,128]{1,0:T(8,128)S(1)}, f32[40,128]{1,0:T(8,128)S(1)}, u32[]{:S(2)}, u32[]{:S(2)}) %collective-permute-start.4) | collective-permute-done | bytes 20512 | tf_op jit(solution)/shard_map/ppermute | solution.py:376
  22.5 2.6 %collective-permute-start.5 = (f32[40,128]{1,0:T(8,128)S(1)}, f32[40,128]{1,0:T(8,128)S(1)}, u32[]{:S(2)}, u32[]{:S(2)}) collective-permute-start(f32[40,128]{1,0:T(8,128)S(1)} %get-tuple-element.33.back_minus), channel_id=1, source_target_pairs={{0,4},{4,8},{8,12},{12,16},{16,20},{20,24},{24,28},{28,0},{1,5},{5... | collective-permute-start | bytes 61448 | tf_op jit(solution)/shard_map/ppermute | solution.py:376
  25.1 1.4 %shard_map.93._.refs_5_ = f32[3,1024,128]{2,1,0:T(8,128)S(1)} custom-call(f32[1024,128]{1,0:T(8,128)S(1)} %get-tuple-element.26.refs_0_.press, f32[1024,128]{1,0:T(8,128)S(1)} %get-tuple-element.27.refs_1_.depth, f32[2,1024,128]{2,1,0:T(8,128)S(1)} %get-tuple-element.28.refs_2_.sat, f32[3,1024,128]{2,1,0:T(8,128)S(1)} %bitcast.12, ...), custom_call_target="tpu_custom_call", output_to_operand_aliasing={{}: (5, {})} | custom-call | flops 8000000 | bytes 125000 | tf_op jit(solution)/shard_map/pallas_call | solution.py:450
  26.5 2.8 %collective-permute-done.5.from_down = f32[40,128]{1,0:T(8,128)S(1)} collective-permute-done((f32[40,128]{1,0:T(8,128)S(1)}, f32[40,128]{1,0:T(8,128)S(1)}, u32[]{:S(2)}, u32[]{:S(2)}) %collective-permute-start.5) | collective-permute-done | bytes 20512 | tf_op jit(solution)/shard_map/ppermute | solution.py:376
  29.3 0.0 collective-permute-start.6
  29.3 0.0 collective-permute-done.8.hxa
  29.3 0.5 %collective-permute-start.7 = (f32[40,128]{1,0:T(8,128)S(1)}, f32[40,128]{1,0:T(8,128)S(1)}, u32[]{:S(2)}, u32[]{:S(2)}) collective-permute-start(f32[40,128]{1,0:T(8,128)S(1)} %get-tuple-element.35), channel_id=1, source_target_pairs={{0,3},{1,2},{2,1},{3,0},{4,7},{5,6},{6,5},{7,4},{8,11},{9,10},{10,... | collective-permute-start | bytes 61448 | tf_op jit(solution)/shard_map/ppermute | solution.py:359
  29.8 1.4 %shard_map.94._ = f32[3,1024,128]{2,1,0:T(8,128)S(1)} custom-call(f32[1024,128]{1,0:T(8,128)S(1)} %get-tuple-element.26.refs_0_.press, f32[1024,128]{1,0:T(8,128)S(1)} %get-tuple-element.27.refs_1_.depth, f32[2,1024,128]{2,1,0:T(8,128)S(1)} %get-tuple-element.28.refs_2_.sat, f32[3,1024,128]{2,1,0:T(8,128)S(1)} %bitcast.13, ...), custom_call_target="tpu_custom_call", output_to_operand_aliasing={{}: (5, {})} | custom-call | flops 8000000 | bytes 125000 | tf_op jit(solution)/shard_map/pallas_call | solution.py:450
  31.2 0.0 collective-permute-done.9.hxb
  31.2 0.0 collective-permute-done.10.hya
  31.2 0.0 collective-permute-done.11.hyb
  31.2 0.7 %edge.1._ = f32[3,1024,128]{2,1,0:T(8,128)S(1)} custom-call(f32[64,128]{1,0:T(8,128)S(1)} %get-tuple-element.23.own, f32[64,128]{1,0:T(8,128)S(1)} %collective-permute-done.got_a, f32[64,128]{1,0:T(8,128)S(1)} %collective-permute-done.1.got_b, f32[64,128]{1,0:T(8,128)S(1)} %collective-permute-done.2.plus, ...), custom_call_target="tpu_custom_call", output_to_operand_aliasing={{}: (17, {})} | custom-call | flops 4000000 | bytes 62500 | tf_op jit(solution)/shard_map/edge/pallas_call | solution.py:513
  31.9 0.7 %collective-permute-done.7.from_b = f32[40,128]{1,0:T(8,128)S(1)} collective-permute-done((f32[40,128]{1,0:T(8,128)S(1)}, f32[40,128]{1,0:T(8,128)S(1)}, u32[]{:S(2)}, u32[]{:S(2)}) %collective-permute-start.7) | collective-permute-done | bytes 20512 | tf_op jit(solution)/shard_map/ppermute | solution.py:359
  32.6 1.4 %finish.1 = (f32[3,1024,128]{2,1,0:T(8,128)}, f32[3,1024,128]{2,1,0:T(8,128)S(1)}) custom-call(f32[64,128]{1,0:T(8,128)S(1)} %get-tuple-element.23.own, f32[40,128]{1,0:T(8,128)S(1)} %get-tuple-element.31.back_y._, f32[40,128]{1,0:T(8,128)S(1)} %collective-permute-done.4.from_up, ...), custom_call_target="tpu_custom_call", output_to_operand_aliasing={{1}: (7, {})} | custom-call | flops 2000000 | bytes 31250 | tf_op jit(solution)/shard_map/finish/pallas_call | solution.py:524
  (7 shorter events, 0.0 us)
Async XLA Ops:
  0.0 5.7 %copy-start.1 = (f32[32,32,128]{2,1,0:T(8,128)S(1)}, f32[32,32,128]{2,1,0:T(8,128)}, u32[]{:S(2)}) copy-start(f32[32,32,128]{2,1,0:T(8,128)} %param.13) | copy-start | bytes 1572868
  0.0 5.7 %copy-start = (f32[3,32,32,128]{3,2,1,0:T(8,128)S(1)}, f32[3,32,32,128]{3,2,1,0:T(8,128)}, u32[]{:S(2)}) copy-start(f32[3,32,32,128]{3,2,1,0:T(8,128)} %param.12) | copy-start | bytes 4718596
  2.5 4.5 %collective-permute-start = (f32[64,128]{1,0:T(8,128)S(1)}, f32[64,128]{1,0:T(8,128)S(1)}, u32[]{:S(2)}, u32[]{:S(2)}) collective-permute-start(f32[64,128]{1,0:T(8,128)S(1)} %get-tuple-element.24), channel_id=1, source_target_pairs={{0,1},{1,0},{2,3},{3,2},{4,5},{5,4},{6,7},{7,6},{8,9},{9,8},{10,11... | collective-permute-start | bytes 98312 | tf_op jit(solution)/shard_map/ppermute | solution.py:359
  3.1 4.3 %collective-permute-start.1 = (f32[64,128]{1,0:T(8,128)S(1)}, f32[64,128]{1,0:T(8,128)S(1)}, u32[]{:S(2)}, u32[]{:S(2)}) collective-permute-start(f32[64,128]{1,0:T(8,128)S(1)} %get-tuple-element.25), channel_id=1, source_target_pairs={{0,3},{1,2},{2,1},{3,0},{4,7},{5,6},{6,5},{7,4},{8,11},{9,10},{10,... | collective-permute-start | bytes 98312 | tf_op jit(solution)/shard_map/ppermute | solution.py:359
  7.4 6.7 %collective-permute-start.2 = (f32[64,128]{1,0:T(8,128)S(1)}, f32[64,128]{1,0:T(8,128)S(1)}, u32[]{:S(2)}, u32[]{:S(2)}) collective-permute-start(f32[64,128]{1,0:T(8,128)S(1)} %get-tuple-element.29), channel_id=1, source_target_pairs={{0,4},{4,8},{8,12},{12,16},{16,20},{20,24},{24,28},{28,0},{1,5},{5... | collective-permute-start | bytes 98312 | tf_op jit(solution)/shard_map/ppermute | solution.py:376
  9.0 5.0 %collective-permute-start.3 = (f32[64,128]{1,0:T(8,128)S(1)}, f32[64,128]{1,0:T(8,128)S(1)}, u32[]{:S(2)}, u32[]{:S(2)}) collective-permute-start(f32[64,128]{1,0:T(8,128)S(1)} %get-tuple-element.30), channel_id=1, source_target_pairs={{0,28},{4,0},{8,4},{12,8},{16,12},{20,16},{24,20},{28,24},{1,29},{... | collective-permute-start | bytes 98312 | tf_op jit(solution)/shard_map/ppermute | solution.py:376
  14.4 14.9 %collective-permute-start.8 = (f32[5,32,128]{2,1,0:T(8,128)S(1)}, f32[5,32,128]{2,1,0:T(8,128)S(1)}, u32[]{:S(2)}, u32[]{:S(2)}) collective-permute-start(f32[5,32,128]{2,1,0:T(8,128)S(1)} %get-tuple-element.36), channel_id=1, source_target_pairs={{0,4},{4,0},{8,12},{12,8},{16,20},{20,16},{24,28},{28,24},{1,5},{5... | collective-permute-start | bytes 245768 | tf_op jit(solution)/shard_map/ppermute | solution.py:359
  15.8 15.4 %collective-permute-start.9 = (f32[5,32,128]{2,1,0:T(8,128)S(1)}, f32[5,32,128]{2,1,0:T(8,128)S(1)}, u32[]{:S(2)}, u32[]{:S(2)}) collective-permute-start(f32[5,32,128]{2,1,0:T(8,128)S(1)} %get-tuple-element.37), channel_id=1, source_target_pairs={{0,1},{1,0},{2,3},{3,2},{4,8},{5,9},{6,10},{7,11},{8,4},{9,5},{10,... | collective-permute-start | bytes 245768 | tf_op jit(solution)/shard_map/ppermute | solution.py:371
  15.8 15.4 %collective-permute-start.10 = (f32[5,32,128]{2,1,0:T(8,128)S(1)}, f32[5,32,128]{2,1,0:T(8,128)S(1)}, u32[]{:S(2)}, u32[]{:S(2)}) collective-permute-start(f32[5,32,128]{2,1,0:T(8,128)S(1)} %get-tuple-element.38), channel_id=1, source_target_pairs={{0,1},{1,0},{2,3},{3,2},{4,5},{5,4},{6,7},{7,6},{8,9},{9,8},{10,11... | collective-permute-start | bytes 245768 | tf_op jit(solution)/shard_map/ppermute | solution.py:359
  16.3 14.9 %collective-permute-start.11 = (f32[5,32,128]{2,1,0:T(8,128)S(1)}, f32[5,32,128]{2,1,0:T(8,128)S(1)}, u32[]{:S(2)}, u32[]{:S(2)}) collective-permute-start(f32[5,32,128]{2,1,0:T(8,128)S(1)} %get-tuple-element.39), channel_id=1, source_target_pairs={{0,3},{1,2},{2,1},{3,0},{4,7},{5,6},{6,5},{7,4},{8,11},{9,10},{10,... | collective-permute-start | bytes 245768 | tf_op jit(solution)/shard_map/ppermute | solution.py:359
  17.4 5.1 %collective-permute-start.4 = (f32[40,128]{1,0:T(8,128)S(1)}, f32[40,128]{1,0:T(8,128)S(1)}, u32[]{:S(2)}, u32[]{:S(2)}) collective-permute-start(f32[40,128]{1,0:T(8,128)S(1)} %get-tuple-element.32.back_plus), channel_id=1, source_target_pairs={{0,28},{4,0},{8,4},{12,8},{16,12},{20,16},{24,20},{28,24},{1,29},{... | collective-permute-start | bytes 61448 | tf_op jit(solution)/shard_map/ppermute | solution.py:376
  22.5 6.8 %collective-permute-start.5 = (f32[40,128]{1,0:T(8,128)S(1)}, f32[40,128]{1,0:T(8,128)S(1)}, u32[]{:S(2)}, u32[]{:S(2)}) collective-permute-start(f32[40,128]{1,0:T(8,128)S(1)} %get-tuple-element.33.back_minus), channel_id=1, source_target_pairs={{0,4},{4,8},{8,12},{12,16},{16,20},{20,24},{24,28},{28,0},{1,5},{5... | collective-permute-start | bytes 61448 | tf_op jit(solution)/shard_map/ppermute | solution.py:376
  29.3 2.6 %collective-permute-start.6 = (f32[40,128]{1,0:T(8,128)S(1)}, f32[40,128]{1,0:T(8,128)S(1)}, u32[]{:S(2)}, u32[]{:S(2)}) collective-permute-start(f32[40,128]{1,0:T(8,128)S(1)} %get-tuple-element.34), channel_id=1, source_target_pairs={{0,1},{1,0},{2,3},{3,2},{4,5},{5,4},{6,7},{7,6},{8,9},{9,8},{10,11... | collective-permute-start | bytes 61448 | tf_op jit(solution)/shard_map/ppermute | solution.py:359
  29.3 3.3 %collective-permute-start.7 = (f32[40,128]{1,0:T(8,128)S(1)}, f32[40,128]{1,0:T(8,128)S(1)}, u32[]{:S(2)}, u32[]{:S(2)}) collective-permute-start(f32[40,128]{1,0:T(8,128)S(1)} %get-tuple-element.35), channel_id=1, source_target_pairs={{0,3},{1,2},{2,1},{3,0},{4,7},{5,6},{6,5},{7,4},{8,11},{9,10},{10,... | collective-permute-start | bytes 61448 | tf_op jit(solution)/shard_map/ppermute | solution.py:359
where the time goes:
time: 34.2 us; the launch traced here: 34 us
  starting transfers between devices  17.7 us (52%)
  Pallas kernels  9.56 us (28%)
  waiting for transfers between devices  5.82 us (17%)
  between operations  0.92 us (3%)
    ppermute x4, starting transfers between devices, shifted(): lax.ppermute(value, axis, [(i, (i + step) % count) for i in range(count)])  11 us
    ppermute x7, starting transfers between devices, swapped(): return lax.ppermute(value, axis, route)  6.72 us
    pallas_call x4, Pallas kernels, stencil(): pl.pallas_call(functools.partial(stencil_kernel, cx, cy, first, last), in...  5.42 us
    ppermute x4, waiting for transfers between devices, shifted(): lax.ppermute(value, axis, [(i, (i + step) % count) for i in range(count)])  4.8 us
    pallas_call x1, Pallas kernels, step(): pl.pallas_call(functools.partial(pack_kernel, nx, ny), in_specs=[spec(HBM...  1.71 us
    pallas_call x1, Pallas kernels, step(): pl.pallas_call(finish_kernel, in_specs=[spec(VMEM)] * 8, out_specs=[spec(...  1.43 us
    ppermute x7, waiting for transfers between devices, swapped(): return lax.ppermute(value, axis, route)  1.02 us
  transfers between devices with their start and end apart: 12, of which 5 were waited for; matrix products, arithmetic and copies ran while one was open for 0% of the time, Pallas kernels for 18%

commit v1 on v0

--- a/solution.py
+++ b/solution.py
@@ -152,11 +152,21 @@
     return (press[rows, :], depth[rows, :]) + mobility(water, oil), water, oil
 
 
-def stencil_kernel(cx, cy, first, last, *refs):
-    if first == 0:
-        press, depth, sat, perm, pore, out = refs
-    else:
-        press, depth, sat, perm, pore, _, out = refs
+def chosen(role):
+    if role is None:
+        return True
+    return (lax.axis_index("gx") == 0) == role
+
+
+def stencil_kernel(cx, cy, first, last, role, *refs):
+    @pl.when(chosen(role))
+    def _():
+        stencil_rows(cx, cy, first, last, *refs)
+
+
+def stencil_rows(cx, cy, first, last, *refs):
+    press, depth, sat, perm, pore = refs[:5]
+    out = refs[-1]
     lanes = press.shape[1]
     lane = lax.broadcasted_iota(jnp.int32, (8, lanes), 1)
     sub = lax.broadcasted_iota(jnp.int32, (8, lanes), 0)
@@ -218,12 +228,12 @@
             carry += flow_x(first - 1, c, low)
         carry = tuple(carry)
     end = min(last, cx - 1)
-    carry = lax.fori_loop(first, end, lambda a, value: one_row(a, value, False), carry)
+    carry = lax.fori_loop(first, end, lambda a, value: one_row(a, value, False), carry, unroll=2)
     if last == cx:
         one_row(cx - 1, carry, True)
 
 
-def halo_kernel(cx, cy, press, depth, sat, perm, _, hxa, hxb, hya, hyb):
+def halo_kernel(cx, cy, press, depth, sat, perm, hxa, hxb, hya, hyb):
     even_x = lax.rem(lax.axis_index("gx"), 2) == 0
     even_y = lax.rem(lax.axis_index("gy"), 2) == 0
     columns = cx * cy
@@ -282,7 +292,13 @@
         out[3 * FLOW : BACK, :] = jnp.zeros((BACK - 3 * FLOW, out.shape[1]), jnp.float32)
 
 
-def edge_kernel(
+def edge_kernel(nx, ny, cx, cy, role, *refs):
+    @pl.when(chosen(role))
+    def _():
+        edge_cells(nx, ny, cx, cy, *refs)
+
+
+def edge_cells(
     nx, ny, cx, cy,
     own, got_a, got_b, plus, minus, back_plus, back_minus, back_y,
     hxa, hxb, hya, hyb, press, depth, sat, perm, pore, _,
@@ -376,7 +392,7 @@
     return lax.ppermute(value, axis, [(i, (i + step) % count) for i in range(count)])
 
 
-def relay_kernel(own, got_a, got_b, _, plus, minus):
+def relay_kernel(own, got_a, got_b, plus, minus):
     parts = (own, got_a, got_b)
     for tx, out in ((1, plus), (2, minus)):
         low = tx * BLOCK
@@ -442,36 +458,58 @@
     )))
     perm, pore = flat(permeability), flat(pore_volume)
 
-    cuts = tuple(cx * k // 4 for k in range(5))
-
-    def stencil(part, base):
-        first, last = cuts[part], cuts[part + 1]
-        operands = [press, deep, sat, perm, pore] + ([] if first == 0 else [base])
+    cuts = (cx // 4, cx * 5 // 8)
+
+    def stencil(first, last, role, base):
+        operands = [press, deep, sat, perm, pore] + ([] if base is None else [base])
         return pl.pallas_call(
-            functools.partial(stencil_kernel, cx, cy, first, last),
-            in_specs=[spec(VMEM)] * 5 + ([] if first == 0 else [spec(pl.ANY)]),
+            functools.partial(stencil_kernel, cx, cy, first, last, role),
+            in_specs=[spec(VMEM)] * 5 + ([] if base is None else [spec(pl.ANY)]),
             out_specs=spec(VMEM),
             out_shape=full,
-            input_output_aliases={} if first == 0 else {5: 0},
+            input_output_aliases={} if base is None else {5: 0},
             compiler_params=params(),
             cost_estimate=cost(8_000_000 * (last - first) // 8),
+            name="stencil",
         )(*operands)
 
+    def edges(role, base):
+        return pl.pallas_call(
+            functools.partial(edge_kernel, nx, ny, cx, cy, role),
+            in_specs=[spec(VMEM)] * 18,
+            out_specs=spec(VMEM),
+            out_shape=full,
+            input_output_aliases={17: 0},
+            compiler_params=params(),
+            cost_estimate=cost(4_000_000),
+            name="edge",
+        )(own, got_a, got_b, plus, minus, back_plus, back_minus, back_y,
+          hxa, hxb, hya, hyb, press, deep, sat, perm, pore, base)
+
+    got_b = swapped(msg_b, "gy", 1)
     got_a = swapped(msg_a, "gy", 0)
-    got_b = swapped(msg_b, "gy", 1)
-    base = stencil(0, None)
+    base = stencil(0, cuts[0], None, None)
+    hxa, hxb, hya, hyb = pl.pallas_call(
+        functools.partial(halo_kernel, cx, cy),
+        in_specs=[spec(VMEM)] * 4,
+        out_specs=[spec(VMEM)] * 4,
+        out_shape=[halo_x] * 2 + [halo_y] * 2,
+        compiler_params=params(),
+        cost_estimate=cost(100_000),
+        name="halo",
+    )(press, deep, sat, perm)
     plus, minus = pl.pallas_call(
         relay_kernel,
-        in_specs=[spec(VMEM)] * 3 + [spec(pl.ANY)],
+        in_specs=[spec(VMEM)] * 3,
         out_specs=[spec(VMEM)] * 2,
         out_shape=[message] * 2,
         compiler_params=params(),
         cost_estimate=cost(100_000),
         name="relay",
-    )(own, got_a, got_b, base)
+    )(own, got_a, got_b)
     plus = shifted(plus, "gx", 1)
     minus = shifted(minus, "gx", -1)
-    base = stencil(1, base)
+    base = stencil(cuts[0], cuts[1], None, base)
     back_plus, back_minus, back_y = pl.pallas_call(
         fault_kernel,
         in_specs=[spec(VMEM)] * 8 + [spec(pl.ANY)],
@@ -483,21 +521,13 @@
         name="fault",
     )(own, got_a, got_b, plus, minus, press, deep, sat, base)
     from_down = shifted(back_minus, "gx", 1)
+    base = stencil(cuts[1], cx, True, base)
     from_up = shifted(back_plus, "gx", -1)
-    hxa, hxb, hya, hyb = pl.pallas_call(
-        functools.partial(halo_kernel, cx, cy),
-        in_specs=[spec(VMEM)] * 4 + [spec(pl.ANY)],
-        out_specs=[spec(VMEM)] * 4,
-        out_shape=[halo_x] * 2 + [halo_y] * 2,
-        compiler_params=params(),
-        cost_estimate=cost(100_000),
-        name="halo",
-    )(press, deep, sat, perm, back_y)
     hxa = swapped(hxa, "gx", 0)
     hxb = swapped_inside(hxb)
+    hyb = swapped(hyb, "gy", 1)
     hya = swapped(hya, "gy", 0)
-    hyb = swapped(hyb, "gy", 1)
-    base = stencil(2, base)
+    base = stencil(cuts[1], cx, False, base)
     back_a, back_b = pl.pallas_call(
         relay_back_kernel,
         in_specs=[spec(VMEM)] * 3 + [spec(pl.ANY)],
@@ -507,20 +537,9 @@
         cost_estimate=cost(100_000),
         name="relay_back",
     )(back_y, from_up, from_down, base)
+    from_b = swapped(back_b, "gy", 1)
     from_a = swapped(back_a, "gy", 0)
-    from_b = swapped(back_b, "gy", 1)
-    base = stencil(3, base)
-    base = pl.pallas_call(
-        functools.partial(edge_kernel, nx, ny, cx, cy),
-        in_specs=[spec(VMEM)] * 18,
-        out_specs=spec(VMEM),
-        out_shape=full,
-        input_output_aliases={17: 0},
-        compiler_params=params(),
-        cost_estimate=cost(4_000_000),
-        name="edge",
-    )(own, got_a, got_b, plus, minus, back_plus, back_minus, back_y,
-      hxa, hxb, hya, hyb, press, deep, sat, perm, pore, base)
+    base = edges(None, base)
     out, _ = pl.pallas_call(
         finish_kernel,
         in_specs=[spec(VMEM)] * 8,

time: 34.2 us -> 34.3 us (level)
  waiting for transfers between devices: 5.82 us -> 9.45 us
  Pallas kernels: 9.56 us -> 7.42 us
  starting transfers between devices: 17.7 us -> 16.3 us
    ppermute x4, starting transfers between devices: 11 us -> 8.3 us  [shifted(): lax.ppermute(value, axis, [(i, (i + step) % count) for i in range(count)])]
    pallas_call x6, Pallas kernels: 6.1 us -> 3.96 us  [the longest x4 3.28 us: stencil(): pl.pallas_call(functools.partial(stencil_kernel, cx, cy, first, last, rol...]
    ppermute x4, waiting for transfers between devices: 4.8 us -> 6.8 us  [shifted(): lax.ppermute(value, axis, [(i, (i + step) % count) for i in range(count)])]
    ppermute x7, waiting for transfers between devices: 1.02 us -> 2.65 us  [swapped(): return lax.ppermute(value, axis, route)]
    ppermute x7, starting transfers between devices: 6.72 us -> 8.05 us  [swapped(): return lax.ppermute(value, axis, route)]
  transfers between devices with their start and end apart: 12 -> 12, of which waited for: 5 -> 4; matrix products, arithmetic and copies ran while one was open for 0% -> 0% of each run, Pallas kernels for 18% -> 13%
where the time goes in v1:
time: 34.3 us; the launch traced here: 34.1 us
  starting transfers between devices  16.3 us (48%)
  waiting for transfers between devices  9.45 us (28%)
  Pallas kernels  7.42 us (22%)
  between operations  0.87 us (3%)
    ppermute x4, starting transfers between devices, shifted(): lax.ppermute(value, axis, [(i, (i + step) % count) for i in range(count)])  8.3 us
    ppermute x7, starting transfers between devices, swapped(): return lax.ppermute(value, axis, route)  8.05 us
    ppermute x4, waiting for transfers between devices, shifted(): lax.ppermute(value, axis, [(i, (i + step) % count) for i in range(count)])  6.8 us
    pallas_call x4, Pallas kernels, stencil(): pl.pallas_call(functools.partial(stencil_kernel, cx, cy, first, last, rol...  3.28 us
    ppermute x7, waiting for transfers between devices, swapped(): return lax.ppermute(value, axis, route)  2.65 us
    pallas_call x1, Pallas kernels, step(): pl.pallas_call(functools.partial(pack_kernel, nx, ny), in_specs=[spec(HBM...  1.71 us
    pallas_call x1, Pallas kernels, step(): pl.pallas_call(finish_kernel, in_specs=[spec(VMEM)] * 8, out_specs=[spec(...  1.43 us
  transfers between devices with their start and end apart: 12, of which 4 were waited for; matrix products, arithmetic and copies ran while one was open for 0% of the time, Pallas kernels for 13%

profile of v1, /device:TPU:0, one launch (start us, length us, event | category | flops | bytes accessed | tf_op | source)
XLA Modules:
  0.0 34.1 jit_solution(2763200204963976002)
XLA Ops:
  0.8 1.7 %pack.1 = (f32[64,128]{1,0:T(8,128)S(1)}, f32[64,128]{1,0:T(8,128)S(1)}, f32[64,128]{1,0:T(8,128)S(1)}, f32[1024,128]{1,0:T(8,128)S(1)}, f32[1024,128]{1,0:T(8,128)S(1)}, /*index=5*/f32[2,1024,128]{2,1,0:T(8,128)S(1)}) custom-call(s32[3,32]{1,0:T(4,128)} %bitcast.24, s32[32]{0:T(128)} %kind_ref.1, s32[1,1]{1,0:T(1,128)} %bitcast.8.count_ref, ...), custom_call_target="tpu_custom_call" | custom-call | flops 4000000 | bytes 62500 | tf_op jit(solution)/shard_map/pack/pallas_call | solution.py:438
  2.5 0.6 %collective-permute-start = (f32[64,128]{1,0:T(8,128)S(1)}, f32[64,128]{1,0:T(8,128)S(1)}, u32[]{:S(2)}, u32[]{:S(2)}) collective-permute-start(f32[64,128]{1,0:T(8,128)S(1)} %get-tuple-element.24), channel_id=1, source_target_pairs={{0,1},{1,0},{2,3},{3,2},{4,5},{5,4},{6,7},{7,6},{8,9},{9,8},{10,11... | collective-permute-start | bytes 98312 | tf_op jit(solution)/shard_map/ppermute | solution.py:375
  3.0 2.6 %collective-permute-start.1 = (f32[64,128]{1,0:T(8,128)S(1)}, f32[64,128]{1,0:T(8,128)S(1)}, u32[]{:S(2)}, u32[]{:S(2)}) collective-permute-start(f32[64,128]{1,0:T(8,128)S(1)} %get-tuple-element.25), channel_id=1, source_target_pairs={{0,3},{1,2},{2,1},{3,0},{4,7},{5,6},{6,5},{7,4},{8,11},{9,10},{10,... | collective-permute-start | bytes 98312 | tf_op jit(solution)/shard_map/ppermute | solution.py:375
  5.7 0.0 collective-permute-done.got_a.refs_1_
  5.7 1.7 %collective-permute-done.1.got_b.refs_2_ = f32[64,128]{1,0:T(8,128)S(1)} collective-permute-done((f32[64,128]{1,0:T(8,128)S(1)}, f32[64,128]{1,0:T(8,128)S(1)}, u32[]{:S(2)}, u32[]{:S(2)}) %collective-permute-start.1) | collective-permute-done | bytes 32800 | tf_op jit(solution)/shard_map/ppermute | solution.py:375
  7.4 1.6 %collective-permute-start.2 = (f32[64,128]{1,0:T(8,128)S(1)}, f32[64,128]{1,0:T(8,128)S(1)}, u32[]{:S(2)}, u32[]{:S(2)}) collective-permute-start(f32[64,128]{1,0:T(8,128)S(1)} %get-tuple-element.26), channel_id=1, source_target_pairs={{0,4},{4,8},{8,12},{12,16},{16,20},{20,24},{24,28},{28,0},{1,5},{5... | collective-permute-start | bytes 98312 | tf_op jit(solution)/shard_map/ppermute | solution.py:392
  9.0 0.1 halo.1
  9.1 1.6 %collective-permute-start.8 = (f32[5,32,128]{2,1,0:T(8,128)S(1)}, f32[5,32,128]{2,1,0:T(8,128)S(1)}, u32[]{:S(2)}, u32[]{:S(2)}) collective-permute-start(f32[5,32,128]{2,1,0:T(8,128)S(1)} %get-tuple-element.36), channel_id=1, source_target_pairs={{0,4},{4,0},{8,12},{12,8},{16,20},{20,16},{24,28},{28,24},{1,5},{5... | collective-permute-start | bytes 245768 | tf_op jit(solution)/shard_map/ppermute | solution.py:375
  10.7 3.5 %collective-permute-start.3 = (f32[64,128]{1,0:T(8,128)S(1)}, f32[64,128]{1,0:T(8,128)S(1)}, u32[]{:S(2)}, u32[]{:S(2)}) collective-permute-start(f32[64,128]{1,0:T(8,128)S(1)} %get-tuple-element.27), channel_id=1, source_target_pairs={{0,28},{4,0},{8,4},{12,8},{16,12},{20,16},{24,20},{28,24},{1,29},{... | collective-permute-start | bytes 98312 | tf_op jit(solution)/shard_map/ppermute | solution.py:392
  14.2 0.0 collective-permute-start.9
  14.3 0.5 %collective-permute-start.10 = (f32[5,32,128]{2,1,0:T(8,128)S(1)}, f32[5,32,128]{2,1,0:T(8,128)S(1)}, u32[]{:S(2)}, u32[]{:S(2)}) collective-permute-start(f32[5,32,128]{2,1,0:T(8,128)S(1)} %get-tuple-element.38), channel_id=1, source_target_pairs={{0,1},{1,0},{2,3},{3,2},{4,5},{5,4},{6,7},{7,6},{8,9},{9,8},{10,11... | collective-permute-start | bytes 245768 | tf_op jit(solution)/shard_map/ppermute | solution.py:375
  14.8 0.0 collective-permute-done.2.plus.refs_3_
  14.8 1.1 %collective-permute-start.11 = (f32[5,32,128]{2,1,0:T(8,128)S(1)}, f32[5,32,128]{2,1,0:T(8,128)S(1)}, u32[]{:S(2)}, u32[]{:S(2)}) collective-permute-start(f32[5,32,128]{2,1,0:T(8,128)S(1)} %get-tuple-element.39), channel_id=1, source_target_pairs={{0,3},{1,2},{2,1},{3,0},{4,7},{5,6},{6,5},{7,4},{8,11},{9,10},{10,... | collective-permute-start | bytes 245768 | tf_op jit(solution)/shard_map/ppermute | solution.py:375
  15.9 0.8 %stencil.4.refs_5_ = f32[3,1024,128]{2,1,0:T(8,128)S(1)} custom-call(f32[1024,128]{1,0:T(8,128)S(1)} %get-tuple-element.28.refs_0_.press.refs_12_, f32[1024,128]{1,0:T(8,128)S(1)} %get-tuple-element.29.refs_1_.depth.refs_13_, f32[2,1024,128]{2,1,0:T(8,128)S(1)} %get-tuple-element.30.refs_2_.sat.refs_14_, f32[3,1024,128]{2,1,0:T(8,128)S(1)} %bitcast.10, ...), custom_call_target="tpu_custom_call" | custom-call | flops 8000000 | bytes 125000 | tf_op jit(solution)/shard_map/stencil/pallas_call | solution.py:465
  16.7 1.2 %stencil.5._.refs_5_ = f32[3,1024,128]{2,1,0:T(8,128)S(1)} custom-call(f32[1024,128]{1,0:T(8,128)S(1)} %get-tuple-element.28.refs_0_.press.refs_12_, f32[1024,128]{1,0:T(8,128)S(1)} %get-tuple-element.29.refs_1_.depth.refs_13_, f32[2,1024,128]{2,1,0:T(8,128)S(1)} %get-tuple-element.30.refs_2_.sat.refs_14_, ...), custom_call_target="tpu_custom_call", output_to_operand_aliasing={{}: (5, {})} | custom-call | flops 12000000 | bytes 187500 | tf_op jit(solution)/shard_map/stencil/pallas_call | solution.py:465
  17.9 0.0 collective-permute-done.3.minus.refs_4_
  18.0 0.2 fault.1
  18.2 3.0 %collective-permute-start.4 = (f32[40,128]{1,0:T(8,128)S(1)}, f32[40,128]{1,0:T(8,128)S(1)}, u32[]{:S(2)}, u32[]{:S(2)}) collective-permute-start(f32[40,128]{1,0:T(8,128)S(1)} %get-tuple-element.32.refs_5_), channel_id=1, source_target_pairs={{0,28},{4,0},{8,4},{12,8},{16,12},{20,16},{24,20},{28,24},{1,29},{... | collective-permute-start | bytes 61448 | tf_op jit(solution)/shard_map/ppermute | solution.py:392
  21.1 1.5 %collective-permute-done.4.from_up = f32[40,128]{1,0:T(8,128)S(1)} collective-permute-done((f32[40,128]{1,0:T(8,128)S(1)}, f32[40,128]{1,0:T(8,128)S(1)}, u32[]{:S(2)}, u32[]{:S(2)}) %collective-permute-start.4) | collective-permute-done | bytes 20512 | tf_op jit(solution)/shard_map/ppermute | solution.py:392
  22.6 0.2 collective-permute-start.5
  22.8 1.2 %stencil.6.refs_5_ = f32[3,1024,128]{2,1,0:T(8,128)S(1)} custom-call(f32[1024,128]{1,0:T(8,128)S(1)} %get-tuple-element.28.refs_0_.press.refs_12_, f32[1024,128]{1,0:T(8,128)S(1)} %get-tuple-element.29.refs_1_.depth.refs_13_, f32[2,1024,128]{2,1,0:T(8,128)S(1)} %get-tuple-element.30.refs_2_.sat.refs_14_, ...), custom_call_target="tpu_custom_call", output_to_operand_aliasing={{}: (5, {})} | custom-call | flops 12000000 | bytes 187500 | tf_op jit(solution)/shard_map/stencil/pallas_call | solution.py:465
  24.1 5.3 %collective-permute-done.5.from_down = f32[40,128]{1,0:T(8,128)S(1)} collective-permute-done((f32[40,128]{1,0:T(8,128)S(1)}, f32[40,128]{1,0:T(8,128)S(1)}, u32[]{:S(2)}, u32[]{:S(2)}) %collective-permute-start.5) | collective-permute-done | bytes 20512 | tf_op jit(solution)/shard_map/ppermute | solution.py:392
  29.4 0.0 collective-permute-start.6
  29.4 0.0 collective-permute-done.8.refs_8_
  29.4 1.6 %collective-permute-start.7 = (f32[40,128]{1,0:T(8,128)S(1)}, f32[40,128]{1,0:T(8,128)S(1)}, u32[]{:S(2)}, u32[]{:S(2)}) collective-permute-start(f32[40,128]{1,0:T(8,128)S(1)} %get-tuple-element.35), channel_id=1, source_target_pairs={{0,3},{1,2},{2,1},{3,0},{4,7},{5,6},{6,5},{7,4},{8,11},{9,10},{10,... | collective-permute-start | bytes 61448 | tf_op jit(solution)/shard_map/ppermute | solution.py:375
  31.0 0.0 collective-permute-done.9.refs_9_
  31.0 0.0 collective-permute-done.10.refs_10_
  31.0 0.0 collective-permute-done.11.refs_11_
  31.0 0.7 %edge.1._ = f32[3,1024,128]{2,1,0:T(8,128)S(1)} custom-call(f32[64,128]{1,0:T(8,128)S(1)} %get-tuple-element.23.own.refs_0_, f32[64,128]{1,0:T(8,128)S(1)} %collective-permute-done.got_a.refs_1_, f32[64,128]{1,0:T(8,128)S(1)} %collective-permute-done.1.got_b.refs_2_, ...), custom_call_target="tpu_custom_call", output_to_operand_aliasing={{}: (17, {})} | custom-call | flops 4000000 | bytes 62500 | tf_op jit(solution)/shard_map/edge/pallas_call | solution.py:477
  31.7 0.0 collective-permute-done.6.from_a
  31.7 1.0 %collective-permute-done.7.from_b = f32[40,128]{1,0:T(8,128)S(1)} collective-permute-done((f32[40,128]{1,0:T(8,128)S(1)}, f32[40,128]{1,0:T(8,128)S(1)}, u32[]{:S(2)}, u32[]{:S(2)}) %collective-permute-start.7) | collective-permute-done | bytes 20512 | tf_op jit(solution)/shard_map/ppermute | solution.py:375
  32.7 1.4 %finish.1 = (f32[3,1024,128]{2,1,0:T(8,128)}, f32[3,1024,128]{2,1,0:T(8,128)S(1)}) custom-call(f32[64,128]{1,0:T(8,128)S(1)} %get-tuple-element.23.own.refs_0_, f32[40,128]{1,0:T(8,128)S(1)} %get-tuple-element.31.back_y.refs_7_, f32[40,128]{1,0:T(8,128)S(1)} %collective-permute-done.4.from_up, ...), custom_call_target="tpu_custom_call", output_to_operand_aliasing={{1}: (7, {})} | custom-call | flops 2000000 | bytes 31250 | tf_op jit(solution)/shard_map/finish/pallas_call | solution.py:543
  (7 shorter events, 0.0 us)
Async XLA Ops:
  0.0 9.0 %copy-start = (f32[3,32,32,128]{3,2,1,0:T(8,128)S(1)}, f32[3,32,32,128]{3,2,1,0:T(8,128)}, u32[]{:S(2)}) copy-start(f32[3,32,32,128]{3,2,1,0:T(8,128)} %param.12) | copy-start | bytes 4718596
  2.5 3.2 %collective-permute-start = (f32[64,128]{1,0:T(8,128)S(1)}, f32[64,128]{1,0:T(8,128)S(1)}, u32[]{:S(2)}, u32[]{:S(2)}) collective-permute-start(f32[64,128]{1,0:T(8,128)S(1)} %get-tuple-element.24), channel_id=1, source_target_pairs={{0,1},{1,0},{2,3},{3,2},{4,5},{5,4},{6,7},{7,6},{8,9},{9,8},{10,11... | collective-permute-start | bytes 98312 | tf_op jit(solution)/shard_map/ppermute | solution.py:375
  3.0 4.3 %collective-permute-start.1 = (f32[64,128]{1,0:T(8,128)S(1)}, f32[64,128]{1,0:T(8,128)S(1)}, u32[]{:S(2)}, u32[]{:S(2)}) collective-permute-start(f32[64,128]{1,0:T(8,128)S(1)} %get-tuple-element.25), channel_id=1, source_target_pairs={{0,3},{1,2},{2,1},{3,0},{4,7},{5,6},{6,5},{7,4},{8,11},{9,10},{10,... | collective-permute-start | bytes 98312 | tf_op jit(solution)/shard_map/ppermute | solution.py:375
  7.4 7.4 %collective-permute-start.2 = (f32[64,128]{1,0:T(8,128)S(1)}, f32[64,128]{1,0:T(8,128)S(1)}, u32[]{:S(2)}, u32[]{:S(2)}) collective-permute-start(f32[64,128]{1,0:T(8,128)S(1)} %get-tuple-element.26), channel_id=1, source_target_pairs={{0,4},{4,8},{8,12},{12,16},{16,20},{20,24},{24,28},{28,0},{1,5},{5... | collective-permute-start | bytes 98312 | tf_op jit(solution)/shard_map/ppermute | solution.py:392
  9.0 6.9 %copy-start.1 = (f32[32,32,128]{2,1,0:T(8,128)S(1)}, f32[32,32,128]{2,1,0:T(8,128)}, u32[]{:S(2)}) copy-start(f32[32,32,128]{2,1,0:T(8,128)} %param.13) | copy-start | bytes 1572868
  9.1 20.3 %collective-permute-start.8 = (f32[5,32,128]{2,1,0:T(8,128)S(1)}, f32[5,32,128]{2,1,0:T(8,128)S(1)}, u32[]{:S(2)}, u32[]{:S(2)}) collective-permute-start(f32[5,32,128]{2,1,0:T(8,128)S(1)} %get-tuple-element.36), channel_id=1, source_target_pairs={{0,4},{4,0},{8,12},{12,8},{16,20},{20,16},{24,28},{28,24},{1,5},{5... | collective-permute-start | bytes 245768 | tf_op jit(solution)/shard_map/ppermute | solution.py:375
  10.7 7.2 %collective-permute-start.3 = (f32[64,128]{1,0:T(8,128)S(1)}, f32[64,128]{1,0:T(8,128)S(1)}, u32[]{:S(2)}, u32[]{:S(2)}) collective-permute-start(f32[64,128]{1,0:T(8,128)S(1)} %get-tuple-element.27), channel_id=1, source_target_pairs={{0,28},{4,0},{8,4},{12,8},{16,12},{20,16},{24,20},{28,24},{1,29},{... | collective-permute-start | bytes 98312 | tf_op jit(solution)/shard_map/ppermute | solution.py:392
  14.2 16.8 %collective-permute-start.9 = (f32[5,32,128]{2,1,0:T(8,128)S(1)}, f32[5,32,128]{2,1,0:T(8,128)S(1)}, u32[]{:S(2)}, u32[]{:S(2)}) collective-permute-start(f32[5,32,128]{2,1,0:T(8,128)S(1)} %get-tuple-element.37), channel_id=1, source_target_pairs={{0,1},{1,0},{2,3},{3,2},{4,8},{5,9},{6,10},{7,11},{8,4},{9,5},{10,... | collective-permute-start | bytes 245768 | tf_op jit(solution)/shard_map/ppermute | solution.py:387
  14.3 16.8 %collective-permute-start.10 = (f32[5,32,128]{2,1,0:T(8,128)S(1)}, f32[5,32,128]{2,1,0:T(8,128)S(1)}, u32[]{:S(2)}, u32[]{:S(2)}) collective-permute-start(f32[5,32,128]{2,1,0:T(8,128)S(1)} %get-tuple-element.38), channel_id=1, source_target_pairs={{0,1},{1,0},{2,3},{3,2},{4,5},{5,4},{6,7},{7,6},{8,9},{9,8},{10,11... | collective-permute-start | bytes 245768 | tf_op jit(solution)/shard_map/ppermute | solution.py:375
  14.8 16.3 %collective-permute-start.11 = (f32[5,32,128]{2,1,0:T(8,128)S(1)}, f32[5,32,128]{2,1,0:T(8,128)S(1)}, u32[]{:S(2)}, u32[]{:S(2)}) collective-permute-start(f32[5,32,128]{2,1,0:T(8,128)S(1)} %get-tuple-element.39), channel_id=1, source_target_pairs={{0,3},{1,2},{2,1},{3,0},{4,7},{5,6},{6,5},{7,4},{8,11},{9,10},{10,... | collective-permute-start | bytes 245768 | tf_op jit(solution)/shard_map/ppermute | solution.py:375
  18.2 4.4 %collective-permute-start.4 = (f32[40,128]{1,0:T(8,128)S(1)}, f32[40,128]{1,0:T(8,128)S(1)}, u32[]{:S(2)}, u32[]{:S(2)}) collective-permute-start(f32[40,128]{1,0:T(8,128)S(1)} %get-tuple-element.32.refs_5_), channel_id=1, source_target_pairs={{0,28},{4,0},{8,4},{12,8},{16,12},{20,16},{24,20},{28,24},{1,29},{... | collective-permute-start | bytes 61448 | tf_op jit(solution)/shard_map/ppermute | solution.py:392
  22.6 6.8 %collective-permute-start.5 = (f32[40,128]{1,0:T(8,128)S(1)}, f32[40,128]{1,0:T(8,128)S(1)}, u32[]{:S(2)}, u32[]{:S(2)}) collective-permute-start(f32[40,128]{1,0:T(8,128)S(1)} %get-tuple-element.33.refs_6_), channel_id=1, source_target_pairs={{0,4},{4,8},{8,12},{12,16},{16,20},{20,24},{24,28},{28,0},{1,5},{5... | collective-permute-start | bytes 61448 | tf_op jit(solution)/shard_map/ppermute | solution.py:392
  29.4 2.3 %collective-permute-start.6 = (f32[40,128]{1,0:T(8,128)S(1)}, f32[40,128]{1,0:T(8,128)S(1)}, u32[]{:S(2)}, u32[]{:S(2)}) collective-permute-start(f32[40,128]{1,0:T(8,128)S(1)} %get-tuple-element.34), channel_id=1, source_target_pairs={{0,1},{1,0},{2,3},{3,2},{4,5},{5,4},{6,7},{7,6},{8,9},{9,8},{10,11... | collective-permute-start | bytes 61448 | tf_op jit(solution)/shard_map/ppermute | solution.py:375
  29.4 3.3 %collective-permute-start.7 = (f32[40,128]{1,0:T(8,128)S(1)}, f32[40,128]{1,0:T(8,128)S(1)}, u32[]{:S(2)}, u32[]{:S(2)}) collective-permute-start(f32[40,128]{1,0:T(8,128)S(1)} %get-tuple-element.35), channel_id=1, source_target_pairs={{0,3},{1,2},{2,1},{3,0},{4,7},{5,6},{6,5},{7,4},{8,11},{9,10},{10,... | collective-permute-start | bytes 61448 | tf_op jit(solution)/shard_map/ppermute | solution.py:375

commit v2 on v1

--- a/solution.py
+++ b/solution.py
@@ -65,8 +65,8 @@
 def pack_kernel(
     nx, ny,
     pairs_ref, kind_ref, count_ref, table_ref, press_f, depth_f, sat_f,
-    own, msg_a, msg_b, press, depth, sat,
-    pairs_s, kind_s, count_s, slot_s, seen_s, src_s, knd_s, liv_s, lnd_s, table,
+    own, msg_a, msg_b, press, depth, sat, src_s,
+    pairs_s, kind_s, count_s, slot_s, seen_s, knd_s, liv_s, lnd_s, table,
     sem_i, sem_s,
 ):
     ints = [
@@ -343,8 +343,8 @@
                 out[f, pl.ds(col, 1), :] = out[f, pl.ds(col, 1), :] + scale * flows[at : at + 1, :]
 
 
-def finish_kernel(own, back_y, from_up, from_down, from_a, from_b, pore, _, out, work, sem):
-    origin = own[META + 3 : META + 4, :].astype(jnp.int32)
+def finish_kernel(origin, back_y, from_up, from_down, from_a, from_b, pore, _, out, work, sem):
+    slots = []
     for ty in range(3):
         for tx in range(3):
             if ty > 0:
@@ -354,16 +354,17 @@
             else:
                 ref, row = (from_up, from_down)[tx - 1], 0
             for rank in range(CAP):
-                col = origin[0, (ty * 3 + tx) * CAP + rank]
-                scale = STEP / pore[pl.ds(col, 1), :]
-                for f in range(3):
-                    at = row + f * CAP + rank
-                    work[f, pl.ds(col, 1), :] = (
-                        work[f, pl.ds(col, 1), :] - scale * ref[at : at + 1, :]
-                    )
-    copy = pltpu.make_async_copy(work, out, sem)
-    copy.start()
-    copy.wait()
+                col = origin[(ty * 3 + tx) * CAP + rank]
+                slots.append((ref, row + rank, pl.ds(col, 1), STEP / pore[pl.ds(col, 1), :]))
+    copies = []
+    for f in range(3):
+        for ref, row, col, scale in slots:
+            at = row + f * CAP
+            work[f, col, :] = work[f, col, :] - scale * ref[at : at + 1, :]
+        copies.append(pltpu.make_async_copy(work.at[f], out.at[f], sem.at[f]))
+        copies[-1].start()
+    for copy in copies:
+        copy.wait()
 
 
 def swapped(value, axis, kind):
@@ -435,16 +436,16 @@
 
     message, back, full = vmem(ROWS, layers), vmem(BACK, layers), vmem(3, columns, layers)
     halo_x, halo_y = vmem(5, cy, layers), vmem(5, cx, layers)
-    own, msg_a, msg_b, press, deep, sat = pl.pallas_call(
+    own, msg_a, msg_b, press, deep, sat, origin = pl.pallas_call(
         functools.partial(pack_kernel, nx, ny),
         in_specs=[spec(HBM)] * 7,
-        out_specs=[spec(VMEM)] * 6,
+        out_specs=[spec(VMEM)] * 6 + [spec(SMEM)],
         out_shape=[message] * 3
-        + [vmem(columns, layers)] * 2 + [vmem(2, columns, layers)],
+        + [vmem(columns, layers)] * 2 + [vmem(2, columns, layers)] + [SMEM((slots,), jnp.int32)],
         scratch_shapes=[
             SMEM((3, rows), jnp.int32), SMEM((rows,), jnp.int32), SMEM((1, 1), jnp.int32),
             SMEM((nx * ny,), jnp.int32),
-            SMEM((slots,), jnp.int32), SMEM((slots,), jnp.int32), SMEM((slots,), jnp.int32),
+            SMEM((slots,), jnp.int32), SMEM((slots,), jnp.int32),
             SMEM((slots,), jnp.int32), SMEM((slots,), jnp.int32),
             VMEM(fault_table.shape, f32),
             pltpu.SemaphoreType.DMA((4,)), pltpu.SemaphoreType.DMA((3,)),
@@ -542,15 +543,15 @@
     base = edges(None, base)
     out, _ = pl.pallas_call(
         finish_kernel,
-        in_specs=[spec(VMEM)] * 8,
+        in_specs=[spec(SMEM)] + [spec(VMEM)] * 7,
         out_specs=[spec(HBM), spec(VMEM)],
         out_shape=[jax.ShapeDtypeStruct((3, columns, layers), f32), full],
         input_output_aliases={7: 1},
-        scratch_shapes=[pltpu.SemaphoreType.DMA],
+        scratch_shapes=[pltpu.SemaphoreType.DMA((3,))],
         compiler_params=params(),
         cost_estimate=cost(2_000_000),
         name="finish",
-    )(own, back_y, from_up, from_down, from_a, from_b, pore, base)
+    )(origin, back_y, from_up, from_down, from_a, from_b, pore, base)
     return cells(out)
 
 

time: 34.3 us -> 34.1 us (level)
  no operation moved by 1% of the time
where the time goes in v2:
time: 34.1 us; the launch traced here: 34 us
  starting transfers between devices  16.3 us (48%)
  waiting for transfers between devices  9.45 us (28%)
  Pallas kernels  7.3 us (21%)
  between operations  0.87 us (3%)
    ppermute x4, starting transfers between devices, shifted(): lax.ppermute(value, axis, [(i, (i + step) % count) for i in range(count)])  8.3 us
    ppermute x7, starting transfers between devices, swapped(): return lax.ppermute(value, axis, route)  8.05 us
    ppermute x4, waiting for transfers between devices, shifted(): lax.ppermute(value, axis, [(i, (i + step) % count) for i in range(count)])  6.8 us
    pallas_call x4, Pallas kernels, stencil(): pl.pallas_call(functools.partial(stencil_kernel, cx, cy, first, last, rol...  3.28 us
    ppermute x7, waiting for transfers between devices, swapped(): return lax.ppermute(value, axis, route)  2.65 us
    pallas_call x1, Pallas kernels, step(): pl.pallas_call(functools.partial(pack_kernel, nx, ny), in_specs=[spec(HBM...  1.71 us
    pallas_call x1, Pallas kernels, step(): pl.pallas_call(finish_kernel, in_specs=[spec(SMEM)] + [spec(VMEM)] * 7, o...  1.31 us
  transfers between devices with their start and end apart: 12, of which 4 were waited for; matrix products, arithmetic and copies ran while one was open for 0% of the time, Pallas kernels for 13%

profile of v2, /device:TPU:0, one launch (start us, length us, event | category | flops | bytes accessed | tf_op | source)
XLA Modules:
  0.0 34.0 jit_solution(6031318250151924263)
XLA Ops:
  0.8 1.7 %pack.1 = (f32[64,128]{1,0:T(8,128)S(1)}, f32[64,128]{1,0:T(8,128)S(1)}, f32[64,128]{1,0:T(8,128)S(1)}, f32[1024,128]{1,0:T(8,128)S(1)}, f32[1024,128]{1,0:T(8,1...) custom-call(s32[3,32]{1,0:T(4,128)} %bitcast.24, s32[32]{0:T(128)} %kind_ref.1, s32[1,1]{1,0:T(1,128)} %bitcast.8.count_ref, ...), custom_call_target="tpu_custom_call" | custom-call | flops 4000000 | bytes 62500 | tf_op jit(solution)/shard_map/pack/pallas_call | solution.py:439
  2.5 0.6 %collective-permute-start = (f32[64,128]{1,0:T(8,128)S(1)}, f32[64,128]{1,0:T(8,128)S(1)}, u32[]{:S(2)}, u32[]{:S(2)}) collective-permute-start(f32[64,128]{1,0:T(8,128)S(1)} %get-tuple-element.26), channel_id=1, source_target_pairs={{0,1},{1,0},{2,3},{3,2},{4,5},{5,4},{6,7},{7,6},{8,9},{9,8},{10,11... | collective-permute-start | bytes 98312 | tf_op jit(solution)/shard_map/ppermute | solution.py:376
  3.0 2.6 %collective-permute-start.1 = (f32[64,128]{1,0:T(8,128)S(1)}, f32[64,128]{1,0:T(8,128)S(1)}, u32[]{:S(2)}, u32[]{:S(2)}) collective-permute-start(f32[64,128]{1,0:T(8,128)S(1)} %get-tuple-element.27), channel_id=1, source_target_pairs={{0,3},{1,2},{2,1},{3,0},{4,7},{5,6},{6,5},{7,4},{8,11},{9,10},{10,... | collective-permute-start | bytes 98312 | tf_op jit(solution)/shard_map/ppermute | solution.py:376
  5.7 0.0 collective-permute-done.got_a.refs_1_
  5.7 1.7 %collective-permute-done.1.got_b.refs_2_ = f32[64,128]{1,0:T(8,128)S(1)} collective-permute-done((f32[64,128]{1,0:T(8,128)S(1)}, f32[64,128]{1,0:T(8,128)S(1)}, u32[]{:S(2)}, u32[]{:S(2)}) %collective-permute-start.1) | collective-permute-done | bytes 32800 | tf_op jit(solution)/shard_map/ppermute | solution.py:376
  7.4 1.6 %collective-permute-start.2 = (f32[64,128]{1,0:T(8,128)S(1)}, f32[64,128]{1,0:T(8,128)S(1)}, u32[]{:S(2)}, u32[]{:S(2)}) collective-permute-start(f32[64,128]{1,0:T(8,128)S(1)} %get-tuple-element.28), channel_id=1, source_target_pairs={{0,4},{4,8},{8,12},{12,16},{16,20},{20,24},{24,28},{28,0},{1,5},{5... | collective-permute-start | bytes 98312 | tf_op jit(solution)/shard_map/ppermute | solution.py:393
  9.0 0.1 halo.1
  9.1 1.6 %collective-permute-start.8 = (f32[5,32,128]{2,1,0:T(8,128)S(1)}, f32[5,32,128]{2,1,0:T(8,128)S(1)}, u32[]{:S(2)}, u32[]{:S(2)}) collective-permute-start(f32[5,32,128]{2,1,0:T(8,128)S(1)} %get-tuple-element.38), channel_id=1, source_target_pairs={{0,4},{4,0},{8,12},{12,8},{16,20},{20,16},{24,28},{28,24},{1,5},{5... | collective-permute-start | bytes 245768 | tf_op jit(solution)/shard_map/ppermute | solution.py:376
  10.7 3.5 %collective-permute-start.3 = (f32[64,128]{1,0:T(8,128)S(1)}, f32[64,128]{1,0:T(8,128)S(1)}, u32[]{:S(2)}, u32[]{:S(2)}) collective-permute-start(f32[64,128]{1,0:T(8,128)S(1)} %get-tuple-element.29), channel_id=1, source_target_pairs={{0,28},{4,0},{8,4},{12,8},{16,12},{20,16},{24,20},{28,24},{1,29},{... | collective-permute-start | bytes 98312 | tf_op jit(solution)/shard_map/ppermute | solution.py:393
  14.2 0.0 collective-permute-start.9
  14.3 0.5 %collective-permute-start.10 = (f32[5,32,128]{2,1,0:T(8,128)S(1)}, f32[5,32,128]{2,1,0:T(8,128)S(1)}, u32[]{:S(2)}, u32[]{:S(2)}) collective-permute-start(f32[5,32,128]{2,1,0:T(8,128)S(1)} %get-tuple-element.40), channel_id=1, source_target_pairs={{0,1},{1,0},{2,3},{3,2},{4,5},{5,4},{6,7},{7,6},{8,9},{9,8},{10,11... | collective-permute-start | bytes 245768 | tf_op jit(solution)/shard_map/ppermute | solution.py:376
  14.8 0.0 collective-permute-done.2.plus.refs_3_
  14.8 1.1 %collective-permute-start.11 = (f32[5,32,128]{2,1,0:T(8,128)S(1)}, f32[5,32,128]{2,1,0:T(8,128)S(1)}, u32[]{:S(2)}, u32[]{:S(2)}) collective-permute-start(f32[5,32,128]{2,1,0:T(8,128)S(1)} %get-tuple-element.41), channel_id=1, source_target_pairs={{0,3},{1,2},{2,1},{3,0},{4,7},{5,6},{6,5},{7,4},{8,11},{9,10},{10,... | collective-permute-start | bytes 245768 | tf_op jit(solution)/shard_map/ppermute | solution.py:376
  15.9 0.8 %stencil.4.refs_5_ = f32[3,1024,128]{2,1,0:T(8,128)S(1)} custom-call(f32[1024,128]{1,0:T(8,128)S(1)} %get-tuple-element.30.refs_0_.press.refs_12_, f32[1024,128]{1,0:T(8,128)S(1)} %get-tuple-element.31.refs_1_.depth.refs_13_, f32[2,1024,128]{2,1,0:T(8,128)S(1)} %get-tuple-element.32.refs_2_.sat.refs_14_, f32[3,1024,128]{2,1,0:T(8,128)S(1)} %bitcast.10, ...), custom_call_target="tpu_custom_call" | custom-call | flops 8000000 | bytes 125000 | tf_op jit(solution)/shard_map/stencil/pallas_call | solution.py:466
  16.7 1.2 %stencil.5._.refs_5_ = f32[3,1024,128]{2,1,0:T(8,128)S(1)} custom-call(f32[1024,128]{1,0:T(8,128)S(1)} %get-tuple-element.30.refs_0_.press.refs_12_, f32[1024,128]{1,0:T(8,128)S(1)} %get-tuple-element.31.refs_1_.depth.refs_13_, f32[2,1024,128]{2,1,0:T(8,128)S(1)} %get-tuple-element.32.refs_2_.sat.refs_14_, ...), custom_call_target="tpu_custom_call", output_to_operand_aliasing={{}: (5, {})} | custom-call | flops 12000000 | bytes 187500 | tf_op jit(solution)/shard_map/stencil/pallas_call | solution.py:466
  17.9 0.0 collective-permute-done.3.minus.refs_4_
  18.0 0.2 fault.1
  18.2 3.0 %collective-permute-start.4 = (f32[40,128]{1,0:T(8,128)S(1)}, f32[40,128]{1,0:T(8,128)S(1)}, u32[]{:S(2)}, u32[]{:S(2)}) collective-permute-start(f32[40,128]{1,0:T(8,128)S(1)} %get-tuple-element.34.refs_5_), channel_id=1, source_target_pairs={{0,28},{4,0},{8,4},{12,8},{16,12},{20,16},{24,20},{28,24},{1,29},{... | collective-permute-start | bytes 61448 | tf_op jit(solution)/shard_map/ppermute | solution.py:393
  21.1 1.5 %collective-permute-done.4.from_up = f32[40,128]{1,0:T(8,128)S(1)} collective-permute-done((f32[40,128]{1,0:T(8,128)S(1)}, f32[40,128]{1,0:T(8,128)S(1)}, u32[]{:S(2)}, u32[]{:S(2)}) %collective-permute-start.4) | collective-permute-done | bytes 20512 | tf_op jit(solution)/shard_map/ppermute | solution.py:393
  22.6 0.2 collective-permute-start.5
  22.8 1.2 %stencil.6.refs_5_ = f32[3,1024,128]{2,1,0:T(8,128)S(1)} custom-call(f32[1024,128]{1,0:T(8,128)S(1)} %get-tuple-element.30.refs_0_.press.refs_12_, f32[1024,128]{1,0:T(8,128)S(1)} %get-tuple-element.31.refs_1_.depth.refs_13_, f32[2,1024,128]{2,1,0:T(8,128)S(1)} %get-tuple-element.32.refs_2_.sat.refs_14_, ...), custom_call_target="tpu_custom_call", output_to_operand_aliasing={{}: (5, {})} | custom-call | flops 12000000 | bytes 187500 | tf_op jit(solution)/shard_map/stencil/pallas_call | solution.py:466
  24.1 5.3 %collective-permute-done.5.from_down = f32[40,128]{1,0:T(8,128)S(1)} collective-permute-done((f32[40,128]{1,0:T(8,128)S(1)}, f32[40,128]{1,0:T(8,128)S(1)}, u32[]{:S(2)}, u32[]{:S(2)}) %collective-permute-start.5) | collective-permute-done | bytes 20512 | tf_op jit(solution)/shard_map/ppermute | solution.py:393
  29.4 0.0 collective-permute-start.6
  29.4 0.0 collective-permute-done.8.refs_8_
  29.4 1.6 %collective-permute-start.7 = (f32[40,128]{1,0:T(8,128)S(1)}, f32[40,128]{1,0:T(8,128)S(1)}, u32[]{:S(2)}, u32[]{:S(2)}) collective-permute-start(f32[40,128]{1,0:T(8,128)S(1)} %get-tuple-element.37), channel_id=1, source_target_pairs={{0,3},{1,2},{2,1},{3,0},{4,7},{5,6},{6,5},{7,4},{8,11},{9,10},{10,... | collective-permute-start | bytes 61448 | tf_op jit(solution)/shard_map/ppermute | solution.py:376
  31.0 0.0 collective-permute-done.9.refs_9_
  31.0 0.0 collective-permute-done.10.refs_10_
  31.0 0.0 collective-permute-done.11.refs_11_
  31.0 0.7 %edge.1._ = f32[3,1024,128]{2,1,0:T(8,128)S(1)} custom-call(f32[64,128]{1,0:T(8,128)S(1)} %get-tuple-element.25.own.refs_0_, f32[64,128]{1,0:T(8,128)S(1)} %collective-permute-done.got_a.refs_1_, f32[64,128]{1,0:T(8,128)S(1)} %collective-permute-done.1.got_b.refs_2_, ...), custom_call_target="tpu_custom_call", output_to_operand_aliasing={{}: (17, {})} | custom-call | flops 4000000 | bytes 62500 | tf_op jit(solution)/shard_map/edge/pallas_call | solution.py:478
  31.7 0.0 collective-permute-done.6.from_a
  31.7 1.0 %collective-permute-done.7.from_b = f32[40,128]{1,0:T(8,128)S(1)} collective-permute-done((f32[40,128]{1,0:T(8,128)S(1)}, f32[40,128]{1,0:T(8,128)S(1)}, u32[]{:S(2)}, u32[]{:S(2)}) %collective-permute-start.7) | collective-permute-done | bytes 20512 | tf_op jit(solution)/shard_map/ppermute | solution.py:376
  32.7 1.3 %finish.1 = (f32[3,1024,128]{2,1,0:T(8,128)}, f32[3,1024,128]{2,1,0:T(8,128)S(1)}) custom-call(s32[36]{0:T(128)S(4)} %get-tuple-element.24.origin, f32[40,128]{1,0:T(8,128)S(1)} %get-tuple-element.33.back_y.refs_7_, f32[40,128]{1,0:T(8,128)S(1)} %collective-permute-done.4.from_up, ...), custom_call_target="tpu_custom_call", output_to_operand_aliasing={{1}: (7, {})} | custom-call | flops 2000000 | bytes 31250 | tf_op jit(solution)/shard_map/finish/pallas_call | solution.py:544
  (7 shorter events, 0.0 us)
Async XLA Ops:
  0.0 9.0 %copy-start = (f32[3,32,32,128]{3,2,1,0:T(8,128)S(1)}, f32[3,32,32,128]{3,2,1,0:T(8,128)}, u32[]{:S(2)}) copy-start(f32[3,32,32,128]{3,2,1,0:T(8,128)} %param.12) | copy-start | bytes 4718596
  2.5 3.2 %collective-permute-start = (f32[64,128]{1,0:T(8,128)S(1)}, f32[64,128]{1,0:T(8,128)S(1)}, u32[]{:S(2)}, u32[]{:S(2)}) collective-permute-start(f32[64,128]{1,0:T(8,128)S(1)} %get-tuple-element.26), channel_id=1, source_target_pairs={{0,1},{1,0},{2,3},{3,2},{4,5},{5,4},{6,7},{7,6},{8,9},{9,8},{10,11... | collective-permute-start | bytes 98312 | tf_op jit(solution)/shard_map/ppermute | solution.py:376
  3.0 4.3 %collective-permute-start.1 = (f32[64,128]{1,0:T(8,128)S(1)}, f32[64,128]{1,0:T(8,128)S(1)}, u32[]{:S(2)}, u32[]{:S(2)}) collective-permute-start(f32[64,128]{1,0:T(8,128)S(1)} %get-tuple-element.27), channel_id=1, source_target_pairs={{0,3},{1,2},{2,1},{3,0},{4,7},{5,6},{6,5},{7,4},{8,11},{9,10},{10,... | collective-permute-start | bytes 98312 | tf_op jit(solution)/shard_map/ppermute | solution.py:376
  7.4 7.4 %collective-permute-start.2 = (f32[64,128]{1,0:T(8,128)S(1)}, f32[64,128]{1,0:T(8,128)S(1)}, u32[]{:S(2)}, u32[]{:S(2)}) collective-permute-start(f32[64,128]{1,0:T(8,128)S(1)} %get-tuple-element.28), channel_id=1, source_target_pairs={{0,4},{4,8},{8,12},{12,16},{16,20},{20,24},{24,28},{28,0},{1,5},{5... | collective-permute-start | bytes 98312 | tf_op jit(solution)/shard_map/ppermute | solution.py:393
  9.0 6.9 %copy-start.1 = (f32[32,32,128]{2,1,0:T(8,128)S(1)}, f32[32,32,128]{2,1,0:T(8,128)}, u32[]{:S(2)}) copy-start(f32[32,32,128]{2,1,0:T(8,128)} %param.13) | copy-start | bytes 1572868
  9.1 20.3 %collective-permute-start.8 = (f32[5,32,128]{2,1,0:T(8,128)S(1)}, f32[5,32,128]{2,1,0:T(8,128)S(1)}, u32[]{:S(2)}, u32[]{:S(2)}) collective-permute-start(f32[5,32,128]{2,1,0:T(8,128)S(1)} %get-tuple-element.38), channel_id=1, source_target_pairs={{0,4},{4,0},{8,12},{12,8},{16,20},{20,16},{24,28},{28,24},{1,5},{5... | collective-permute-start | bytes 245768 | tf_op jit(solution)/shard_map/ppermute | solution.py:376
  10.7 7.2 %collective-permute-start.3 = (f32[64,128]{1,0:T(8,128)S(1)}, f32[64,128]{1,0:T(8,128)S(1)}, u32[]{:S(2)}, u32[]{:S(2)}) collective-permute-start(f32[64,128]{1,0:T(8,128)S(1)} %get-tuple-element.29), channel_id=1, source_target_pairs={{0,28},{4,0},{8,4},{12,8},{16,12},{20,16},{24,20},{28,24},{1,29},{... | collective-permute-start | bytes 98312 | tf_op jit(solution)/shard_map/ppermute | solution.py:393
  14.2 16.8 %collective-permute-start.9 = (f32[5,32,128]{2,1,0:T(8,128)S(1)}, f32[5,32,128]{2,1,0:T(8,128)S(1)}, u32[]{:S(2)}, u32[]{:S(2)}) collective-permute-start(f32[5,32,128]{2,1,0:T(8,128)S(1)} %get-tuple-element.39), channel_id=1, source_target_pairs={{0,1},{1,0},{2,3},{3,2},{4,8},{5,9},{6,10},{7,11},{8,4},{9,5},{10,... | collective-permute-start | bytes 245768 | tf_op jit(solution)/shard_map/ppermute | solution.py:388
  14.3 16.8 %collective-permute-start.10 = (f32[5,32,128]{2,1,0:T(8,128)S(1)}, f32[5,32,128]{2,1,0:T(8,128)S(1)}, u32[]{:S(2)}, u32[]{:S(2)}) collective-permute-start(f32[5,32,128]{2,1,0:T(8,128)S(1)} %get-tuple-element.40), channel_id=1, source_target_pairs={{0,1},{1,0},{2,3},{3,2},{4,5},{5,4},{6,7},{7,6},{8,9},{9,8},{10,11... | collective-permute-start | bytes 245768 | tf_op jit(solution)/shard_map/ppermute | solution.py:376
  14.8 16.3 %collective-permute-start.11 = (f32[5,32,128]{2,1,0:T(8,128)S(1)}, f32[5,32,128]{2,1,0:T(8,128)S(1)}, u32[]{:S(2)}, u32[]{:S(2)}) collective-permute-start(f32[5,32,128]{2,1,0:T(8,128)S(1)} %get-tuple-element.41), channel_id=1, source_target_pairs={{0,3},{1,2},{2,1},{3,0},{4,7},{5,6},{6,5},{7,4},{8,11},{9,10},{10,... | collective-permute-start | bytes 245768 | tf_op jit(solution)/shard_map/ppermute | solution.py:376
  18.2 4.4 %collective-permute-start.4 = (f32[40,128]{1,0:T(8,128)S(1)}, f32[40,128]{1,0:T(8,128)S(1)}, u32[]{:S(2)}, u32[]{:S(2)}) collective-permute-start(f32[40,128]{1,0:T(8,128)S(1)} %get-tuple-element.34.refs_5_), channel_id=1, source_target_pairs={{0,28},{4,0},{8,4},{12,8},{16,12},{20,16},{24,20},{28,24},{1,29},{... | collective-permute-start | bytes 61448 | tf_op jit(solution)/shard_map/ppermute | solution.py:393
  22.6 6.8 %collective-permute-start.5 = (f32[40,128]{1,0:T(8,128)S(1)}, f32[40,128]{1,0:T(8,128)S(1)}, u32[]{:S(2)}, u32[]{:S(2)}) collective-permute-start(f32[40,128]{1,0:T(8,128)S(1)} %get-tuple-element.35.refs_6_), channel_id=1, source_target_pairs={{0,4},{4,8},{8,12},{12,16},{16,20},{20,24},{24,28},{28,0},{1,5},{5... | collective-permute-start | bytes 61448 | tf_op jit(solution)/shard_map/ppermute | solution.py:393
  29.4 2.3 %collective-permute-start.6 = (f32[40,128]{1,0:T(8,128)S(1)}, f32[40,128]{1,0:T(8,128)S(1)}, u32[]{:S(2)}, u32[]{:S(2)}) collective-permute-start(f32[40,128]{1,0:T(8,128)S(1)} %get-tuple-element.36), channel_id=1, source_target_pairs={{0,1},{1,0},{2,3},{3,2},{4,5},{5,4},{6,7},{7,6},{8,9},{9,8},{10,11... | collective-permute-start | bytes 61448 | tf_op jit(solution)/shard_map/ppermute | solution.py:376
  29.4 3.3 %collective-permute-start.7 = (f32[40,128]{1,0:T(8,128)S(1)}, f32[40,128]{1,0:T(8,128)S(1)}, u32[]{:S(2)}, u32[]{:S(2)}) collective-permute-start(f32[40,128]{1,0:T(8,128)S(1)} %get-tuple-element.37), channel_id=1, source_target_pairs={{0,3},{1,2},{2,1},{3,0},{4,7},{5,6},{6,5},{7,4},{8,11},{9,10},{10,... | collective-permute-start | bytes 61448 | tf_op jit(solution)/shard_map/ppermute | solution.py:376

commit v3 on v2

--- a/solution.py
+++ b/solution.py
@@ -66,14 +66,14 @@
     nx, ny,
     pairs_ref, kind_ref, count_ref, table_ref, press_f, depth_f, sat_f,
     own, msg_a, msg_b, press, depth, sat, src_s,
-    pairs_s, kind_s, count_s, slot_s, seen_s, knd_s, liv_s, lnd_s, table,
+    pairs_s, kind_s, count_s, slot_s, knd_s, lnd_s, table,
     sem_i, sem_s,
 ):
     ints = [
         pltpu.make_async_copy(pairs_ref, pairs_s, sem_i.at[0]),
         pltpu.make_async_copy(kind_ref, kind_s, sem_i.at[1]),
         pltpu.make_async_copy(count_ref, count_s, sem_i.at[2]),
-        pltpu.make_async_copy(table_ref, table, sem_i.at[3]),
+        pltpu.make_async_copy(table_ref, table.at[pl.ds(0, table_ref.shape[0])], sem_i.at[3]),
     ]
     for copy in ints:
         copy.start()
@@ -96,25 +96,26 @@
                 ty = 0
             else:
                 ty = jnp.where(even_y == (step_y == 1), 1, 2)
-            slot_s[to_x * ny + to_y] = (ty * 3 + tx) * CAP
+            slot_s[to_x * ny + to_y] = ty * 3 + tx
+    kinds = table_ref.shape[0]
+    table[kinds:, :] = jnp.zeros((table.shape[0] - kinds, table.shape[1]), jnp.float32)
     for k in range(9 * CAP):
-        seen_s[k] = 0
         src_s[k] = 0
-        knd_s[k] = 0
-        liv_s[k] = 0
+        knd_s[k] = kinds
         lnd_s[k] = 0
     for copy in ints:
         copy.wait()
     count = count_s[0, 0]
+    seen = jnp.int32(0)
     for r in range(pairs_s.shape[1]):
-        base = slot_s[pairs_s[1, r]]
-        rank = seen_s[base]
-        seen_s[base] = rank + 1
-        position = base + rank
+        block = slot_s[pairs_s[1, r]]
+        shift = 3 * block
+        rank = lax.shift_right_logical(seen, shift) & 7
+        seen = seen + lax.shift_left(jnp.int32(1), shift)
+        position = block * CAP + rank
         src_s[position] = pairs_s[0, r]
         lnd_s[position] = pairs_s[2, r]
-        knd_s[position] = kind_s[r]
-        liv_s[position] = jnp.where(r < count, 1, 0)
+        knd_s[position] = jnp.where(r < count, kind_s[r], kinds)
     lane = lax.broadcasted_iota(jnp.int32, (1, own.shape[1]), 1)
     messages = (own, msg_a, msg_b)
     origin = jnp.zeros(lane.shape, jnp.int32)
@@ -127,8 +128,7 @@
                 meta = jnp.where(lane == rank, lnd_s[k], meta)
                 origin = jnp.where(lane == k, src_s[k], origin)
                 trans = table[pl.ds(knd_s[k], 1), :]
-                alive = liv_s[k].astype(jnp.float32)
-                out[tx * BLOCK + 4 * CAP + rank : tx * BLOCK + 4 * CAP + rank + 1, :] = trans * alive
+                out[tx * BLOCK + 4 * CAP + rank : tx * BLOCK + 4 * CAP + rank + 1, :] = trans
             out[META + tx : META + tx + 1, :] = meta.astype(jnp.float32)
         out[META + 3 : META + 4, :] = jnp.zeros(lane.shape, jnp.float32)
     own[META + 3 : META + 4, :] = origin.astype(jnp.float32)
@@ -446,8 +446,7 @@
             SMEM((3, rows), jnp.int32), SMEM((rows,), jnp.int32), SMEM((1, 1), jnp.int32),
             SMEM((nx * ny,), jnp.int32),
             SMEM((slots,), jnp.int32), SMEM((slots,), jnp.int32),
-            SMEM((slots,), jnp.int32), SMEM((slots,), jnp.int32),
-            VMEM(fault_table.shape, f32),
+            VMEM((fault_table.shape[0] + 8, layers), f32),
             pltpu.SemaphoreType.DMA((4,)), pltpu.SemaphoreType.DMA((3,)),
         ],
         compiler_params=params(),

time: 34.1 us -> 34.1 us (level)
  no operation moved by 1% of the time
where the time goes in v3:
time: 34.1 us; the launch traced here: 34 us
  starting transfers between devices  16.3 us (48%)
  waiting for transfers between devices  9.45 us (28%)
  Pallas kernels  7.3 us (21%)
  between operations  0.87 us (3%)
    ppermute x4, starting transfers between devices, shifted(): lax.ppermute(value, axis, [(i, (i + step) % count) for i in range(count)])  8.3 us
    ppermute x7, starting transfers between devices, swapped(): return lax.ppermute(value, axis, route)  8.05 us
    ppermute x4, waiting for transfers between devices, shifted(): lax.ppermute(value, axis, [(i, (i + step) % count) for i in range(count)])  6.8 us
    pallas_call x4, Pallas kernels, stencil(): pl.pallas_call(functools.partial(stencil_kernel, cx, cy, first, last, rol...  3.28 us
    ppermute x7, waiting for transfers between devices, swapped(): return lax.ppermute(value, axis, route)  2.65 us
    pallas_call x1, Pallas kernels, step(): pl.pallas_call(functools.partial(pack_kernel, nx, ny), in_specs=[spec(HBM...  1.71 us
    pallas_call x1, Pallas kernels, step(): pl.pallas_call(finish_kernel, in_specs=[spec(SMEM)] + [spec(VMEM)] * 7, o...  1.31 us
  transfers between devices with their start and end apart: 12, of which 4 were waited for; matrix products, arithmetic and copies ran while one was open for 0% of the time, Pallas kernels for 13%

profile of v3, /device:TPU:0, one launch (start us, length us, event | category | flops | bytes accessed | tf_op | source)
XLA Modules:
  0.0 34.0 jit_solution(1605225060177611696)
XLA Ops:
  0.8 1.7 %pack.1 = (f32[64,128]{1,0:T(8,128)S(1)}, f32[64,128]{1,0:T(8,128)S(1)}, f32[64,128]{1,0:T(8,128)S(1)}, f32[1024,128]{1,0:T(8,128)S(1)}, f32[1024,128]{1,0:T(8,1...) custom-call(s32[3,32]{1,0:T(4,128)} %bitcast.24, s32[32]{0:T(128)} %kind_ref.1, s32[1,1]{1,0:T(1,128)} %bitcast.8.count_ref, ...), custom_call_target="tpu_custom_call" | custom-call | flops 4000000 | bytes 62500 | tf_op jit(solution)/shard_map/pack/pallas_call | solution.py:439
  2.5 0.6 %collective-permute-start = (f32[64,128]{1,0:T(8,128)S(1)}, f32[64,128]{1,0:T(8,128)S(1)}, u32[]{:S(2)}, u32[]{:S(2)}) collective-permute-start(f32[64,128]{1,0:T(8,128)S(1)} %get-tuple-element.26), channel_id=1, source_target_pairs={{0,1},{1,0},{2,3},{3,2},{4,5},{5,4},{6,7},{7,6},{8,9},{9,8},{10,11... | collective-permute-start | bytes 98312 | tf_op jit(solution)/shard_map/ppermute | solution.py:376
  3.0 2.6 %collective-permute-start.1 = (f32[64,128]{1,0:T(8,128)S(1)}, f32[64,128]{1,0:T(8,128)S(1)}, u32[]{:S(2)}, u32[]{:S(2)}) collective-permute-start(f32[64,128]{1,0:T(8,128)S(1)} %get-tuple-element.27), channel_id=1, source_target_pairs={{0,3},{1,2},{2,1},{3,0},{4,7},{5,6},{6,5},{7,4},{8,11},{9,10},{10,... | collective-permute-start | bytes 98312 | tf_op jit(solution)/shard_map/ppermute | solution.py:376
  5.7 0.0 collective-permute-done.got_a.refs_1_
  5.7 1.7 %collective-permute-done.1.got_b.refs_2_ = f32[64,128]{1,0:T(8,128)S(1)} collective-permute-done((f32[64,128]{1,0:T(8,128)S(1)}, f32[64,128]{1,0:T(8,128)S(1)}, u32[]{:S(2)}, u32[]{:S(2)}) %collective-permute-start.1) | collective-permute-done | bytes 32800 | tf_op jit(solution)/shard_map/ppermute | solution.py:376
  7.4 1.6 %collective-permute-start.2 = (f32[64,128]{1,0:T(8,128)S(1)}, f32[64,128]{1,0:T(8,128)S(1)}, u32[]{:S(2)}, u32[]{:S(2)}) collective-permute-start(f32[64,128]{1,0:T(8,128)S(1)} %get-tuple-element.28), channel_id=1, source_target_pairs={{0,4},{4,8},{8,12},{12,16},{16,20},{20,24},{24,28},{28,0},{1,5},{5... | collective-permute-start | bytes 98312 | tf_op jit(solution)/shard_map/ppermute | solution.py:393
  9.0 0.1 halo.1
  9.1 1.6 %collective-permute-start.8 = (f32[5,32,128]{2,1,0:T(8,128)S(1)}, f32[5,32,128]{2,1,0:T(8,128)S(1)}, u32[]{:S(2)}, u32[]{:S(2)}) collective-permute-start(f32[5,32,128]{2,1,0:T(8,128)S(1)} %get-tuple-element.38), channel_id=1, source_target_pairs={{0,4},{4,0},{8,12},{12,8},{16,20},{20,16},{24,28},{28,24},{1,5},{5... | collective-permute-start | bytes 245768 | tf_op jit(solution)/shard_map/ppermute | solution.py:376
  10.7 3.5 %collective-permute-start.3 = (f32[64,128]{1,0:T(8,128)S(1)}, f32[64,128]{1,0:T(8,128)S(1)}, u32[]{:S(2)}, u32[]{:S(2)}) collective-permute-start(f32[64,128]{1,0:T(8,128)S(1)} %get-tuple-element.29), channel_id=1, source_target_pairs={{0,28},{4,0},{8,4},{12,8},{16,12},{20,16},{24,20},{28,24},{1,29},{... | collective-permute-start | bytes 98312 | tf_op jit(solution)/shard_map/ppermute | solution.py:393
  14.2 0.0 collective-permute-start.9
  14.3 0.5 %collective-permute-start.10 = (f32[5,32,128]{2,1,0:T(8,128)S(1)}, f32[5,32,128]{2,1,0:T(8,128)S(1)}, u32[]{:S(2)}, u32[]{:S(2)}) collective-permute-start(f32[5,32,128]{2,1,0:T(8,128)S(1)} %get-tuple-element.40), channel_id=1, source_target_pairs={{0,1},{1,0},{2,3},{3,2},{4,5},{5,4},{6,7},{7,6},{8,9},{9,8},{10,11... | collective-permute-start | bytes 245768 | tf_op jit(solution)/shard_map/ppermute | solution.py:376
  14.8 0.0 collective-permute-done.2.plus.refs_3_
  14.8 1.1 %collective-permute-start.11 = (f32[5,32,128]{2,1,0:T(8,128)S(1)}, f32[5,32,128]{2,1,0:T(8,128)S(1)}, u32[]{:S(2)}, u32[]{:S(2)}) collective-permute-start(f32[5,32,128]{2,1,0:T(8,128)S(1)} %get-tuple-element.41), channel_id=1, source_target_pairs={{0,3},{1,2},{2,1},{3,0},{4,7},{5,6},{6,5},{7,4},{8,11},{9,10},{10,... | collective-permute-start | bytes 245768 | tf_op jit(solution)/shard_map/ppermute | solution.py:376
  15.9 0.8 %stencil.4.refs_5_ = f32[3,1024,128]{2,1,0:T(8,128)S(1)} custom-call(f32[1024,128]{1,0:T(8,128)S(1)} %get-tuple-element.30.refs_0_.press.refs_12_, f32[1024,128]{1,0:T(8,128)S(1)} %get-tuple-element.31.refs_1_.depth.refs_13_, f32[2,1024,128]{2,1,0:T(8,128)S(1)} %get-tuple-element.32.refs_2_.sat.refs_14_, f32[3,1024,128]{2,1,0:T(8,128)S(1)} %bitcast.10, ...), custom_call_target="tpu_custom_call" | custom-call | flops 8000000 | bytes 125000 | tf_op jit(solution)/shard_map/stencil/pallas_call | solution.py:465
  16.7 1.2 %stencil.5._.refs_5_ = f32[3,1024,128]{2,1,0:T(8,128)S(1)} custom-call(f32[1024,128]{1,0:T(8,128)S(1)} %get-tuple-element.30.refs_0_.press.refs_12_, f32[1024,128]{1,0:T(8,128)S(1)} %get-tuple-element.31.refs_1_.depth.refs_13_, f32[2,1024,128]{2,1,0:T(8,128)S(1)} %get-tuple-element.32.refs_2_.sat.refs_14_, ...), custom_call_target="tpu_custom_call", output_to_operand_aliasing={{}: (5, {})} | custom-call | flops 12000000 | bytes 187500 | tf_op jit(solution)/shard_map/stencil/pallas_call | solution.py:465
  17.9 0.0 collective-permute-done.3.minus.refs_4_
  18.0 0.2 fault.1
  18.2 3.0 %collective-permute-start.4 = (f32[40,128]{1,0:T(8,128)S(1)}, f32[40,128]{1,0:T(8,128)S(1)}, u32[]{:S(2)}, u32[]{:S(2)}) collective-permute-start(f32[40,128]{1,0:T(8,128)S(1)} %get-tuple-element.34.refs_5_), channel_id=1, source_target_pairs={{0,28},{4,0},{8,4},{12,8},{16,12},{20,16},{24,20},{28,24},{1,29},{... | collective-permute-start | bytes 61448 | tf_op jit(solution)/shard_map/ppermute | solution.py:393
  21.1 1.5 %collective-permute-done.4.from_up = f32[40,128]{1,0:T(8,128)S(1)} collective-permute-done((f32[40,128]{1,0:T(8,128)S(1)}, f32[40,128]{1,0:T(8,128)S(1)}, u32[]{:S(2)}, u32[]{:S(2)}) %collective-permute-start.4) | collective-permute-done | bytes 20512 | tf_op jit(solution)/shard_map/ppermute | solution.py:393
  22.6 0.2 collective-permute-start.5
  22.8 1.2 %stencil.6.refs_5_ = f32[3,1024,128]{2,1,0:T(8,128)S(1)} custom-call(f32[1024,128]{1,0:T(8,128)S(1)} %get-tuple-element.30.refs_0_.press.refs_12_, f32[1024,128]{1,0:T(8,128)S(1)} %get-tuple-element.31.refs_1_.depth.refs_13_, f32[2,1024,128]{2,1,0:T(8,128)S(1)} %get-tuple-element.32.refs_2_.sat.refs_14_, ...), custom_call_target="tpu_custom_call", output_to_operand_aliasing={{}: (5, {})} | custom-call | flops 12000000 | bytes 187500 | tf_op jit(solution)/shard_map/stencil/pallas_call | solution.py:465
  24.1 5.3 %collective-permute-done.5.from_down = f32[40,128]{1,0:T(8,128)S(1)} collective-permute-done((f32[40,128]{1,0:T(8,128)S(1)}, f32[40,128]{1,0:T(8,128)S(1)}, u32[]{:S(2)}, u32[]{:S(2)}) %collective-permute-start.5) | collective-permute-done | bytes 20512 | tf_op jit(solution)/shard_map/ppermute | solution.py:393
  29.4 0.0 collective-permute-start.6
  29.4 0.0 collective-permute-done.8.refs_8_
  29.4 1.6 %collective-permute-start.7 = (f32[40,128]{1,0:T(8,128)S(1)}, f32[40,128]{1,0:T(8,128)S(1)}, u32[]{:S(2)}, u32[]{:S(2)}) collective-permute-start(f32[40,128]{1,0:T(8,128)S(1)} %get-tuple-element.37), channel_id=1, source_target_pairs={{0,3},{1,2},{2,1},{3,0},{4,7},{5,6},{6,5},{7,4},{8,11},{9,10},{10,... | collective-permute-start | bytes 61448 | tf_op jit(solution)/shard_map/ppermute | solution.py:376
  31.0 0.0 collective-permute-done.9.refs_9_
  31.0 0.0 collective-permute-done.10.refs_10_
  31.0 0.0 collective-permute-done.11.refs_11_
  31.0 0.7 %edge.1._ = f32[3,1024,128]{2,1,0:T(8,128)S(1)} custom-call(f32[64,128]{1,0:T(8,128)S(1)} %get-tuple-element.25.own.refs_0_, f32[64,128]{1,0:T(8,128)S(1)} %collective-permute-done.got_a.refs_1_, f32[64,128]{1,0:T(8,128)S(1)} %collective-permute-done.1.got_b.refs_2_, ...), custom_call_target="tpu_custom_call", output_to_operand_aliasing={{}: (17, {})} | custom-call | flops 4000000 | bytes 62500 | tf_op jit(solution)/shard_map/edge/pallas_call | solution.py:477
  31.7 0.0 collective-permute-done.6.from_a
  31.7 1.0 %collective-permute-done.7.from_b = f32[40,128]{1,0:T(8,128)S(1)} collective-permute-done((f32[40,128]{1,0:T(8,128)S(1)}, f32[40,128]{1,0:T(8,128)S(1)}, u32[]{:S(2)}, u32[]{:S(2)}) %collective-permute-start.7) | collective-permute-done | bytes 20512 | tf_op jit(solution)/shard_map/ppermute | solution.py:376
  32.7 1.3 %finish.1 = (f32[3,1024,128]{2,1,0:T(8,128)}, f32[3,1024,128]{2,1,0:T(8,128)S(1)}) custom-call(s32[36]{0:T(128)S(4)} %get-tuple-element.24.origin, f32[40,128]{1,0:T(8,128)S(1)} %get-tuple-element.33.back_y.refs_7_, f32[40,128]{1,0:T(8,128)S(1)} %collective-permute-done.4.from_up, ...), custom_call_target="tpu_custom_call", output_to_operand_aliasing={{1}: (7, {})} | custom-call | flops 2000000 | bytes 31250 | tf_op jit(solution)/shard_map/finish/pallas_call | solution.py:543
  (7 shorter events, 0.0 us)
Async XLA Ops:
  0.0 9.0 %copy-start = (f32[3,32,32,128]{3,2,1,0:T(8,128)S(1)}, f32[3,32,32,128]{3,2,1,0:T(8,128)}, u32[]{:S(2)}) copy-start(f32[3,32,32,128]{3,2,1,0:T(8,128)} %param.12) | copy-start | bytes 4718596
  2.5 3.2 %collective-permute-start = (f32[64,128]{1,0:T(8,128)S(1)}, f32[64,128]{1,0:T(8,128)S(1)}, u32[]{:S(2)}, u32[]{:S(2)}) collective-permute-start(f32[64,128]{1,0:T(8,128)S(1)} %get-tuple-element.26), channel_id=1, source_target_pairs={{0,1},{1,0},{2,3},{3,2},{4,5},{5,4},{6,7},{7,6},{8,9},{9,8},{10,11... | collective-permute-start | bytes 98312 | tf_op jit(solution)/shard_map/ppermute | solution.py:376
  3.0 4.3 %collective-permute-start.1 = (f32[64,128]{1,0:T(8,128)S(1)}, f32[64,128]{1,0:T(8,128)S(1)}, u32[]{:S(2)}, u32[]{:S(2)}) collective-permute-start(f32[64,128]{1,0:T(8,128)S(1)} %get-tuple-element.27), channel_id=1, source_target_pairs={{0,3},{1,2},{2,1},{3,0},{4,7},{5,6},{6,5},{7,4},{8,11},{9,10},{10,... | collective-permute-start | bytes 98312 | tf_op jit(solution)/shard_map/ppermute | solution.py:376
  7.4 7.4 %collective-permute-start.2 = (f32[64,128]{1,0:T(8,128)S(1)}, f32[64,128]{1,0:T(8,128)S(1)}, u32[]{:S(2)}, u32[]{:S(2)}) collective-permute-start(f32[64,128]{1,0:T(8,128)S(1)} %get-tuple-element.28), channel_id=1, source_target_pairs={{0,4},{4,8},{8,12},{12,16},{16,20},{20,24},{24,28},{28,0},{1,5},{5... | collective-permute-start | bytes 98312 | tf_op jit(solution)/shard_map/ppermute | solution.py:393
  9.0 6.9 %copy-start.1 = (f32[32,32,128]{2,1,0:T(8,128)S(1)}, f32[32,32,128]{2,1,0:T(8,128)}, u32[]{:S(2)}) copy-start(f32[32,32,128]{2,1,0:T(8,128)} %param.13) | copy-start | bytes 1572868
  9.1 20.3 %collective-permute-start.8 = (f32[5,32,128]{2,1,0:T(8,128)S(1)}, f32[5,32,128]{2,1,0:T(8,128)S(1)}, u32[]{:S(2)}, u32[]{:S(2)}) collective-permute-start(f32[5,32,128]{2,1,0:T(8,128)S(1)} %get-tuple-element.38), channel_id=1, source_target_pairs={{0,4},{4,0},{8,12},{12,8},{16,20},{20,16},{24,28},{28,24},{1,5},{5... | collective-permute-start | bytes 245768 | tf_op jit(solution)/shard_map/ppermute | solution.py:376
  10.7 7.2 %collective-permute-start.3 = (f32[64,128]{1,0:T(8,128)S(1)}, f32[64,128]{1,0:T(8,128)S(1)}, u32[]{:S(2)}, u32[]{:S(2)}) collective-permute-start(f32[64,128]{1,0:T(8,128)S(1)} %get-tuple-element.29), channel_id=1, source_target_pairs={{0,28},{4,0},{8,4},{12,8},{16,12},{20,16},{24,20},{28,24},{1,29},{... | collective-permute-start | bytes 98312 | tf_op jit(solution)/shard_map/ppermute | solution.py:393
  14.2 16.8 %collective-permute-start.9 = (f32[5,32,128]{2,1,0:T(8,128)S(1)}, f32[5,32,128]{2,1,0:T(8,128)S(1)}, u32[]{:S(2)}, u32[]{:S(2)}) collective-permute-start(f32[5,32,128]{2,1,0:T(8,128)S(1)} %get-tuple-element.39), channel_id=1, source_target_pairs={{0,1},{1,0},{2,3},{3,2},{4,8},{5,9},{6,10},{7,11},{8,4},{9,5},{10,... | collective-permute-start | bytes 245768 | tf_op jit(solution)/shard_map/ppermute | solution.py:388
  14.3 16.8 %collective-permute-start.10 = (f32[5,32,128]{2,1,0:T(8,128)S(1)}, f32[5,32,128]{2,1,0:T(8,128)S(1)}, u32[]{:S(2)}, u32[]{:S(2)}) collective-permute-start(f32[5,32,128]{2,1,0:T(8,128)S(1)} %get-tuple-element.40), channel_id=1, source_target_pairs={{0,1},{1,0},{2,3},{3,2},{4,5},{5,4},{6,7},{7,6},{8,9},{9,8},{10,11... | collective-permute-start | bytes 245768 | tf_op jit(solution)/shard_map/ppermute | solution.py:376
  14.8 16.3 %collective-permute-start.11 = (f32[5,32,128]{2,1,0:T(8,128)S(1)}, f32[5,32,128]{2,1,0:T(8,128)S(1)}, u32[]{:S(2)}, u32[]{:S(2)}) collective-permute-start(f32[5,32,128]{2,1,0:T(8,128)S(1)} %get-tuple-element.41), channel_id=1, source_target_pairs={{0,3},{1,2},{2,1},{3,0},{4,7},{5,6},{6,5},{7,4},{8,11},{9,10},{10,... | collective-permute-start | bytes 245768 | tf_op jit(solution)/shard_map/ppermute | solution.py:376
  18.2 4.4 %collective-permute-start.4 = (f32[40,128]{1,0:T(8,128)S(1)}, f32[40,128]{1,0:T(8,128)S(1)}, u32[]{:S(2)}, u32[]{:S(2)}) collective-permute-start(f32[40,128]{1,0:T(8,128)S(1)} %get-tuple-element.34.refs_5_), channel_id=1, source_target_pairs={{0,28},{4,0},{8,4},{12,8},{16,12},{20,16},{24,20},{28,24},{1,29},{... | collective-permute-start | bytes 61448 | tf_op jit(solution)/shard_map/ppermute | solution.py:393
  22.6 6.8 %collective-permute-start.5 = (f32[40,128]{1,0:T(8,128)S(1)}, f32[40,128]{1,0:T(8,128)S(1)}, u32[]{:S(2)}, u32[]{:S(2)}) collective-permute-start(f32[40,128]{1,0:T(8,128)S(1)} %get-tuple-element.35.refs_6_), channel_id=1, source_target_pairs={{0,4},{4,8},{8,12},{12,16},{16,20},{20,24},{24,28},{28,0},{1,5},{5... | collective-permute-start | bytes 61448 | tf_op jit(solution)/shard_map/ppermute | solution.py:393
  29.4 2.3 %collective-permute-start.6 = (f32[40,128]{1,0:T(8,128)S(1)}, f32[40,128]{1,0:T(8,128)S(1)}, u32[]{:S(2)}, u32[]{:S(2)}) collective-permute-start(f32[40,128]{1,0:T(8,128)S(1)} %get-tuple-element.36), channel_id=1, source_target_pairs={{0,1},{1,0},{2,3},{3,2},{4,5},{5,4},{6,7},{7,6},{8,9},{9,8},{10,11... | collective-permute-start | bytes 61448 | tf_op jit(solution)/shard_map/ppermute | solution.py:376
  29.4 3.3 %collective-permute-start.7 = (f32[40,128]{1,0:T(8,128)S(1)}, f32[40,128]{1,0:T(8,128)S(1)}, u32[]{:S(2)}, u32[]{:S(2)}) collective-permute-start(f32[40,128]{1,0:T(8,128)S(1)} %get-tuple-element.37), channel_id=1, source_target_pairs={{0,3},{1,2},{2,1},{3,0},{4,7},{5,6},{6,5},{7,4},{8,11},{9,10},{10,... | collective-permute-start | bytes 61448 | tf_op jit(solution)/shard_map/ppermute | solution.py:376

commit v4 on v3

--- a/solution.py
+++ b/solution.py
@@ -118,7 +118,6 @@
         knd_s[position] = jnp.where(r < count, kind_s[r], kinds)
     lane = lax.broadcasted_iota(jnp.int32, (1, own.shape[1]), 1)
     messages = (own, msg_a, msg_b)
-    origin = jnp.zeros(lane.shape, jnp.int32)
     for ty in range(3):
         out = messages[ty]
         for tx in range(3):
@@ -126,12 +125,10 @@
             for rank in range(CAP):
                 k = (ty * 3 + tx) * CAP + rank
                 meta = jnp.where(lane == rank, lnd_s[k], meta)
-                origin = jnp.where(lane == k, src_s[k], origin)
                 trans = table[pl.ds(knd_s[k], 1), :]
                 out[tx * BLOCK + 4 * CAP + rank : tx * BLOCK + 4 * CAP + rank + 1, :] = trans
             out[META + tx : META + tx + 1, :] = meta.astype(jnp.float32)
         out[META + 3 : META + 4, :] = jnp.zeros(lane.shape, jnp.float32)
-    own[META + 3 : META + 4, :] = origin.astype(jnp.float32)
     for copy in bulk:
         copy.wait()
     for ty in range(3):
@@ -458,7 +455,7 @@
     )))
     perm, pore = flat(permeability), flat(pore_volume)
 
-    cuts = (cx // 4, cx * 5 // 8)
+    cuts = (cx * 3 // 8, cx * 5 // 8)
 
     def stencil(first, last, role, base):
         operands = [press, deep, sat, perm, pore] + ([] if base is None else [base])

time: 34.1 us -> 34.1 us (level)
  no operation moved by 1% of the time
where the time goes in v4:
time: 34.1 us; the launch traced here: 34 us
  starting transfers between devices  16.3 us (48%)
  waiting for transfers between devices  9.45 us (28%)
  Pallas kernels  7.3 us (21%)
  between operations  0.87 us (3%)
    ppermute x4, starting transfers between devices, shifted(): lax.ppermute(value, axis, [(i, (i + step) % count) for i in range(count)])  8.3 us
    ppermute x7, starting transfers between devices, swapped(): return lax.ppermute(value, axis, route)  8.05 us
    ppermute x4, waiting for transfers between devices, shifted(): lax.ppermute(value, axis, [(i, (i + step) % count) for i in range(count)])  6.8 us
    pallas_call x4, Pallas kernels, stencil(): pl.pallas_call(functools.partial(stencil_kernel, cx, cy, first, last, rol...  3.28 us
    ppermute x7, waiting for transfers between devices, swapped(): return lax.ppermute(value, axis, route)  2.65 us
    pallas_call x1, Pallas kernels, step(): pl.pallas_call(functools.partial(pack_kernel, nx, ny), in_specs=[spec(HBM...  1.71 us
    pallas_call x1, Pallas kernels, step(): pl.pallas_call(finish_kernel, in_specs=[spec(SMEM)] + [spec(VMEM)] * 7, o...  1.31 us
  transfers between devices with their start and end apart: 12, of which 4 were waited for; matrix products, arithmetic and copies ran while one was open for 0% of the time, Pallas kernels for 13%

profile of v4, /device:TPU:0, one launch (start us, length us, event | category | flops | bytes accessed | tf_op | source)
XLA Modules:
  0.0 34.0 jit_solution(7542072865044056945)
XLA Ops:
  0.8 1.7 %pack.1 = (f32[64,128]{1,0:T(8,128)S(1)}, f32[64,128]{1,0:T(8,128)S(1)}, f32[64,128]{1,0:T(8,128)S(1)}, f32[1024,128]{1,0:T(8,128)S(1)}, f32[1024,128]{1,0:T(8,1...) custom-call(s32[3,32]{1,0:T(4,128)} %bitcast.24, s32[32]{0:T(128)} %kind_ref.1, s32[1,1]{1,0:T(1,128)} %bitcast.8.count_ref, ...), custom_call_target="tpu_custom_call" | custom-call | flops 4000000 | bytes 62500 | tf_op jit(solution)/shard_map/pack/pallas_call | solution.py:436
  2.5 0.6 %collective-permute-start = (f32[64,128]{1,0:T(8,128)S(1)}, f32[64,128]{1,0:T(8,128)S(1)}, u32[]{:S(2)}, u32[]{:S(2)}) collective-permute-start(f32[64,128]{1,0:T(8,128)S(1)} %get-tuple-element.26), channel_id=1, source_target_pairs={{0,1},{1,0},{2,3},{3,2},{4,5},{5,4},{6,7},{7,6},{8,9},{9,8},{10,11... | collective-permute-start | bytes 98312 | tf_op jit(solution)/shard_map/ppermute | solution.py:373
  3.0 2.6 %collective-permute-start.1 = (f32[64,128]{1,0:T(8,128)S(1)}, f32[64,128]{1,0:T(8,128)S(1)}, u32[]{:S(2)}, u32[]{:S(2)}) collective-permute-start(f32[64,128]{1,0:T(8,128)S(1)} %get-tuple-element.27), channel_id=1, source_target_pairs={{0,3},{1,2},{2,1},{3,0},{4,7},{5,6},{6,5},{7,4},{8,11},{9,10},{10,... | collective-permute-start | bytes 98312 | tf_op jit(solution)/shard_map/ppermute | solution.py:373
  5.7 0.0 collective-permute-done.got_a.refs_1_
  5.7 1.7 %collective-permute-done.1.got_b.refs_2_ = f32[64,128]{1,0:T(8,128)S(1)} collective-permute-done((f32[64,128]{1,0:T(8,128)S(1)}, f32[64,128]{1,0:T(8,128)S(1)}, u32[]{:S(2)}, u32[]{:S(2)}) %collective-permute-start.1) | collective-permute-done | bytes 32800 | tf_op jit(solution)/shard_map/ppermute | solution.py:373
  7.4 1.6 %collective-permute-start.2 = (f32[64,128]{1,0:T(8,128)S(1)}, f32[64,128]{1,0:T(8,128)S(1)}, u32[]{:S(2)}, u32[]{:S(2)}) collective-permute-start(f32[64,128]{1,0:T(8,128)S(1)} %get-tuple-element.28), channel_id=1, source_target_pairs={{0,4},{4,8},{8,12},{12,16},{16,20},{20,24},{24,28},{28,0},{1,5},{5... | collective-permute-start | bytes 98312 | tf_op jit(solution)/shard_map/ppermute | solution.py:390
  9.0 0.1 halo.1
  9.1 1.6 %collective-permute-start.8 = (f32[5,32,128]{2,1,0:T(8,128)S(1)}, f32[5,32,128]{2,1,0:T(8,128)S(1)}, u32[]{:S(2)}, u32[]{:S(2)}) collective-permute-start(f32[5,32,128]{2,1,0:T(8,128)S(1)} %get-tuple-element.38), channel_id=1, source_target_pairs={{0,4},{4,0},{8,12},{12,8},{16,20},{20,16},{24,28},{28,24},{1,5},{5... | collective-permute-start | bytes 245768 | tf_op jit(solution)/shard_map/ppermute | solution.py:373
  10.7 3.5 %collective-permute-start.3 = (f32[64,128]{1,0:T(8,128)S(1)}, f32[64,128]{1,0:T(8,128)S(1)}, u32[]{:S(2)}, u32[]{:S(2)}) collective-permute-start(f32[64,128]{1,0:T(8,128)S(1)} %get-tuple-element.29), channel_id=1, source_target_pairs={{0,28},{4,0},{8,4},{12,8},{16,12},{20,16},{24,20},{28,24},{1,29},{... | collective-permute-start | bytes 98312 | tf_op jit(solution)/shard_map/ppermute | solution.py:390
  14.2 0.0 collective-permute-start.9
  14.3 0.5 %collective-permute-start.10 = (f32[5,32,128]{2,1,0:T(8,128)S(1)}, f32[5,32,128]{2,1,0:T(8,128)S(1)}, u32[]{:S(2)}, u32[]{:S(2)}) collective-permute-start(f32[5,32,128]{2,1,0:T(8,128)S(1)} %get-tuple-element.40), channel_id=1, source_target_pairs={{0,1},{1,0},{2,3},{3,2},{4,5},{5,4},{6,7},{7,6},{8,9},{9,8},{10,11... | collective-permute-start | bytes 245768 | tf_op jit(solution)/shard_map/ppermute | solution.py:373
  14.8 0.0 collective-permute-done.2.plus.refs_3_
  14.8 1.1 %collective-permute-start.11 = (f32[5,32,128]{2,1,0:T(8,128)S(1)}, f32[5,32,128]{2,1,0:T(8,128)S(1)}, u32[]{:S(2)}, u32[]{:S(2)}) collective-permute-start(f32[5,32,128]{2,1,0:T(8,128)S(1)} %get-tuple-element.41), channel_id=1, source_target_pairs={{0,3},{1,2},{2,1},{3,0},{4,7},{5,6},{6,5},{7,4},{8,11},{9,10},{10,... | collective-permute-start | bytes 245768 | tf_op jit(solution)/shard_map/ppermute | solution.py:373
  15.9 1.2 %stencil.4.refs_5_ = f32[3,1024,128]{2,1,0:T(8,128)S(1)} custom-call(f32[1024,128]{1,0:T(8,128)S(1)} %get-tuple-element.30.refs_0_.press.refs_12_, f32[1024,128]{1,0:T(8,128)S(1)} %get-tuple-element.31.refs_1_.depth.refs_13_, f32[2,1024,128]{2,1,0:T(8,128)S(1)} %get-tuple-element.32.refs_2_.sat.refs_14_, f32[3,1024,128]{2,1,0:T(8,128)S(1)} %bitcast.10, ...), custom_call_target="tpu_custom_call" | custom-call | flops 12000000 | bytes 187500 | tf_op jit(solution)/shard_map/stencil/pallas_call | solution.py:462
  17.1 0.8 %stencil.5._.refs_5_ = f32[3,1024,128]{2,1,0:T(8,128)S(1)} custom-call(f32[1024,128]{1,0:T(8,128)S(1)} %get-tuple-element.30.refs_0_.press.refs_12_, f32[1024,128]{1,0:T(8,128)S(1)} %get-tuple-element.31.refs_1_.depth.refs_13_, f32[2,1024,128]{2,1,0:T(8,128)S(1)} %get-tuple-element.32.refs_2_.sat.refs_14_, ...), custom_call_target="tpu_custom_call", output_to_operand_aliasing={{}: (5, {})} | custom-call | flops 8000000 | bytes 125000 | tf_op jit(solution)/shard_map/stencil/pallas_call | solution.py:462
  17.9 0.0 collective-permute-done.3.minus.refs_4_
  18.0 0.2 fault.1
  18.2 3.0 %collective-permute-start.4 = (f32[40,128]{1,0:T(8,128)S(1)}, f32[40,128]{1,0:T(8,128)S(1)}, u32[]{:S(2)}, u32[]{:S(2)}) collective-permute-start(f32[40,128]{1,0:T(8,128)S(1)} %get-tuple-element.34.refs_5_), channel_id=1, source_target_pairs={{0,28},{4,0},{8,4},{12,8},{16,12},{20,16},{24,20},{28,24},{1,29},{... | collective-permute-start | bytes 61448 | tf_op jit(solution)/shard_map/ppermute | solution.py:390
  21.1 1.5 %collective-permute-done.4.from_up = f32[40,128]{1,0:T(8,128)S(1)} collective-permute-done((f32[40,128]{1,0:T(8,128)S(1)}, f32[40,128]{1,0:T(8,128)S(1)}, u32[]{:S(2)}, u32[]{:S(2)}) %collective-permute-start.4) | collective-permute-done | bytes 20512 | tf_op jit(solution)/shard_map/ppermute | solution.py:390
  22.6 0.2 collective-permute-start.5
  22.8 1.2 %stencil.6.refs_5_ = f32[3,1024,128]{2,1,0:T(8,128)S(1)} custom-call(f32[1024,128]{1,0:T(8,128)S(1)} %get-tuple-element.30.refs_0_.press.refs_12_, f32[1024,128]{1,0:T(8,128)S(1)} %get-tuple-element.31.refs_1_.depth.refs_13_, f32[2,1024,128]{2,1,0:T(8,128)S(1)} %get-tuple-element.32.refs_2_.sat.refs_14_, ...), custom_call_target="tpu_custom_call", output_to_operand_aliasing={{}: (5, {})} | custom-call | flops 12000000 | bytes 187500 | tf_op jit(solution)/shard_map/stencil/pallas_call | solution.py:462
  24.1 5.3 %collective-permute-done.5.from_down = f32[40,128]{1,0:T(8,128)S(1)} collective-permute-done((f32[40,128]{1,0:T(8,128)S(1)}, f32[40,128]{1,0:T(8,128)S(1)}, u32[]{:S(2)}, u32[]{:S(2)}) %collective-permute-start.5) | collective-permute-done | bytes 20512 | tf_op jit(solution)/shard_map/ppermute | solution.py:390
  29.4 0.0 collective-permute-start.6
  29.4 0.0 collective-permute-done.8.refs_8_
  29.4 1.6 %collective-permute-start.7 = (f32[40,128]{1,0:T(8,128)S(1)}, f32[40,128]{1,0:T(8,128)S(1)}, u32[]{:S(2)}, u32[]{:S(2)}) collective-permute-start(f32[40,128]{1,0:T(8,128)S(1)} %get-tuple-element.37), channel_id=1, source_target_pairs={{0,3},{1,2},{2,1},{3,0},{4,7},{5,6},{6,5},{7,4},{8,11},{9,10},{10,... | collective-permute-start | bytes 61448 | tf_op jit(solution)/shard_map/ppermute | solution.py:373
  31.0 0.0 collective-permute-done.9.refs_9_
  31.0 0.0 collective-permute-done.10.refs_10_
  31.0 0.0 collective-permute-done.11.refs_11_
  31.0 0.7 %edge.1._ = f32[3,1024,128]{2,1,0:T(8,128)S(1)} custom-call(f32[64,128]{1,0:T(8,128)S(1)} %get-tuple-element.25.own.refs_0_, f32[64,128]{1,0:T(8,128)S(1)} %collective-permute-done.got_a.refs_1_, f32[64,128]{1,0:T(8,128)S(1)} %collective-permute-done.1.got_b.refs_2_, ...), custom_call_target="tpu_custom_call", output_to_operand_aliasing={{}: (17, {})} | custom-call | flops 4000000 | bytes 62500 | tf_op jit(solution)/shard_map/edge/pallas_call | solution.py:474
  31.7 0.0 collective-permute-done.6.from_a
  31.7 1.0 %collective-permute-done.7.from_b = f32[40,128]{1,0:T(8,128)S(1)} collective-permute-done((f32[40,128]{1,0:T(8,128)S(1)}, f32[40,128]{1,0:T(8,128)S(1)}, u32[]{:S(2)}, u32[]{:S(2)}) %collective-permute-start.7) | collective-permute-done | bytes 20512 | tf_op jit(solution)/shard_map/ppermute | solution.py:373
  32.7 1.3 %finish.1 = (f32[3,1024,128]{2,1,0:T(8,128)}, f32[3,1024,128]{2,1,0:T(8,128)S(1)}) custom-call(s32[36]{0:T(128)S(4)} %get-tuple-element.24.origin, f32[40,128]{1,0:T(8,128)S(1)} %get-tuple-element.33.back_y.refs_7_, f32[40,128]{1,0:T(8,128)S(1)} %collective-permute-done.4.from_up, ...), custom_call_target="tpu_custom_call", output_to_operand_aliasing={{1}: (7, {})} | custom-call | flops 2000000 | bytes 31250 | tf_op jit(solution)/shard_map/finish/pallas_call | solution.py:540
  (7 shorter events, 0.0 us)
Async XLA Ops:
  0.0 9.0 %copy-start = (f32[3,32,32,128]{3,2,1,0:T(8,128)S(1)}, f32[3,32,32,128]{3,2,1,0:T(8,128)}, u32[]{:S(2)}) copy-start(f32[3,32,32,128]{3,2,1,0:T(8,128)} %param.12) | copy-start | bytes 4718596
  2.5 3.2 %collective-permute-start = (f32[64,128]{1,0:T(8,128)S(1)}, f32[64,128]{1,0:T(8,128)S(1)}, u32[]{:S(2)}, u32[]{:S(2)}) collective-permute-start(f32[64,128]{1,0:T(8,128)S(1)} %get-tuple-element.26), channel_id=1, source_target_pairs={{0,1},{1,0},{2,3},{3,2},{4,5},{5,4},{6,7},{7,6},{8,9},{9,8},{10,11... | collective-permute-start | bytes 98312 | tf_op jit(solution)/shard_map/ppermute | solution.py:373
  3.0 4.3 %collective-permute-start.1 = (f32[64,128]{1,0:T(8,128)S(1)}, f32[64,128]{1,0:T(8,128)S(1)}, u32[]{:S(2)}, u32[]{:S(2)}) collective-permute-start(f32[64,128]{1,0:T(8,128)S(1)} %get-tuple-element.27), channel_id=1, source_target_pairs={{0,3},{1,2},{2,1},{3,0},{4,7},{5,6},{6,5},{7,4},{8,11},{9,10},{10,... | collective-permute-start | bytes 98312 | tf_op jit(solution)/shard_map/ppermute | solution.py:373
  7.4 7.4 %collective-permute-start.2 = (f32[64,128]{1,0:T(8,128)S(1)}, f32[64,128]{1,0:T(8,128)S(1)}, u32[]{:S(2)}, u32[]{:S(2)}) collective-permute-start(f32[64,128]{1,0:T(8,128)S(1)} %get-tuple-element.28), channel_id=1, source_target_pairs={{0,4},{4,8},{8,12},{12,16},{16,20},{20,24},{24,28},{28,0},{1,5},{5... | collective-permute-start | bytes 98312 | tf_op jit(solution)/shard_map/ppermute | solution.py:390
  9.0 6.9 %copy-start.1 = (f32[32,32,128]{2,1,0:T(8,128)S(1)}, f32[32,32,128]{2,1,0:T(8,128)}, u32[]{:S(2)}) copy-start(f32[32,32,128]{2,1,0:T(8,128)} %param.13) | copy-start | bytes 1572868
  9.1 20.3 %collective-permute-start.8 = (f32[5,32,128]{2,1,0:T(8,128)S(1)}, f32[5,32,128]{2,1,0:T(8,128)S(1)}, u32[]{:S(2)}, u32[]{:S(2)}) collective-permute-start(f32[5,32,128]{2,1,0:T(8,128)S(1)} %get-tuple-element.38), channel_id=1, source_target_pairs={{0,4},{4,0},{8,12},{12,8},{16,20},{20,16},{24,28},{28,24},{1,5},{5... | collective-permute-start | bytes 245768 | tf_op jit(solution)/shard_map/ppermute | solution.py:373
  10.7 7.2 %collective-permute-start.3 = (f32[64,128]{1,0:T(8,128)S(1)}, f32[64,128]{1,0:T(8,128)S(1)}, u32[]{:S(2)}, u32[]{:S(2)}) collective-permute-start(f32[64,128]{1,0:T(8,128)S(1)} %get-tuple-element.29), channel_id=1, source_target_pairs={{0,28},{4,0},{8,4},{12,8},{16,12},{20,16},{24,20},{28,24},{1,29},{... | collective-permute-start | bytes 98312 | tf_op jit(solution)/shard_map/ppermute | solution.py:390
  14.2 16.8 %collective-permute-start.9 = (f32[5,32,128]{2,1,0:T(8,128)S(1)}, f32[5,32,128]{2,1,0:T(8,128)S(1)}, u32[]{:S(2)}, u32[]{:S(2)}) collective-permute-start(f32[5,32,128]{2,1,0:T(8,128)S(1)} %get-tuple-element.39), channel_id=1, source_target_pairs={{0,1},{1,0},{2,3},{3,2},{4,8},{5,9},{6,10},{7,11},{8,4},{9,5},{10,... | collective-permute-start | bytes 245768 | tf_op jit(solution)/shard_map/ppermute | solution.py:385
  14.3 16.8 %collective-permute-start.10 = (f32[5,32,128]{2,1,0:T(8,128)S(1)}, f32[5,32,128]{2,1,0:T(8,128)S(1)}, u32[]{:S(2)}, u32[]{:S(2)}) collective-permute-start(f32[5,32,128]{2,1,0:T(8,128)S(1)} %get-tuple-element.40), channel_id=1, source_target_pairs={{0,1},{1,0},{2,3},{3,2},{4,5},{5,4},{6,7},{7,6},{8,9},{9,8},{10,11... | collective-permute-start | bytes 245768 | tf_op jit(solution)/shard_map/ppermute | solution.py:373
  14.8 16.3 %collective-permute-start.11 = (f32[5,32,128]{2,1,0:T(8,128)S(1)}, f32[5,32,128]{2,1,0:T(8,128)S(1)}, u32[]{:S(2)}, u32[]{:S(2)}) collective-permute-start(f32[5,32,128]{2,1,0:T(8,128)S(1)} %get-tuple-element.41), channel_id=1, source_target_pairs={{0,3},{1,2},{2,1},{3,0},{4,7},{5,6},{6,5},{7,4},{8,11},{9,10},{10,... | collective-permute-start | bytes 245768 | tf_op jit(solution)/shard_map/ppermute | solution.py:373
  18.2 4.4 %collective-permute-start.4 = (f32[40,128]{1,0:T(8,128)S(1)}, f32[40,128]{1,0:T(8,128)S(1)}, u32[]{:S(2)}, u32[]{:S(2)}) collective-permute-start(f32[40,128]{1,0:T(8,128)S(1)} %get-tuple-element.34.refs_5_), channel_id=1, source_target_pairs={{0,28},{4,0},{8,4},{12,8},{16,12},{20,16},{24,20},{28,24},{1,29},{... | collective-permute-start | bytes 61448 | tf_op jit(solution)/shard_map/ppermute | solution.py:390
  22.6 6.8 %collective-permute-start.5 = (f32[40,128]{1,0:T(8,128)S(1)}, f32[40,128]{1,0:T(8,128)S(1)}, u32[]{:S(2)}, u32[]{:S(2)}) collective-permute-start(f32[40,128]{1,0:T(8,128)S(1)} %get-tuple-element.35.refs_6_), channel_id=1, source_target_pairs={{0,4},{4,8},{8,12},{12,16},{16,20},{20,24},{24,28},{28,0},{1,5},{5... | collective-permute-start | bytes 61448 | tf_op jit(solution)/shard_map/ppermute | solution.py:390
  29.4 2.3 %collective-permute-start.6 = (f32[40,128]{1,0:T(8,128)S(1)}, f32[40,128]{1,0:T(8,128)S(1)}, u32[]{:S(2)}, u32[]{:S(2)}) collective-permute-start(f32[40,128]{1,0:T(8,128)S(1)} %get-tuple-element.36), channel_id=1, source_target_pairs={{0,1},{1,0},{2,3},{3,2},{4,5},{5,4},{6,7},{7,6},{8,9},{9,8},{10,11... | collective-permute-start | bytes 61448 | tf_op jit(solution)/shard_map/ppermute | solution.py:373
  29.4 3.3 %collective-permute-start.7 = (f32[40,128]{1,0:T(8,128)S(1)}, f32[40,128]{1,0:T(8,128)S(1)}, u32[]{:S(2)}, u32[]{:S(2)}) collective-permute-start(f32[40,128]{1,0:T(8,128)S(1)} %get-tuple-element.37), channel_id=1, source_target_pairs={{0,3},{1,2},{2,1},{3,0},{4,7},{5,6},{6,5},{7,4},{8,11},{9,10},{10,... | collective-permute-start | bytes 61448 | tf_op jit(solution)/shard_map/ppermute | solution.py:373
